TPU v7x, 32 devices: a whole 2x2x4 slice. The times are simulated.
32 devices in a mesh: gz: 2 (over core), gx: 4 (over z), gy: 4 (over y, x).
Axes of the slice: x: 2, y: 2, z: 4, core: 2. Of those that a mesh axis runs over, the one named last changes fastest.
Arguments:
- pair_repr: bfloat16 [8, 384, 384, 128], P('gz', 'gx', 'gy'), may hold values from -9 to 9
- seq_lengths: int32 [8], replicated, may hold values from 96 to 384
- weight_in: bfloat16 [128, 640], replicated, may hold values from -0.5 to 0.5
- weight_out: bfloat16 [128, 128], replicated, may hold values from -0.5 to 0.5
Outputs:
- updated: bfloat16 [8, 384, 384, 128], P('gz', 'gx', 'gy')
- magnitude: float32 [], replicated
All inputs are finite; a program needn't handle non-finite values.
Results may differ from a plain program's by a relative error of at most 0.0034.
Values may be sent and summed in bfloat16 or wider, within the bound.
A program may use at most 384 MiB of HBM per device.

v0:
```python
import jax
import jax.numpy as jnp
from jax import lax
from jax.sharding import PartitionSpec as P


def layer_norm(values):
    mean_value = jnp.mean(values, axis=-1, keepdims=True)
    centered = values - mean_value
    variance = jnp.mean(centered * centered, axis=-1, keepdims=True)
    return centered * lax.rsqrt(variance + 1e-05)


def per_device(pair_repr, seq_lengths, weight_in, weight_out):
    batch_dev, row_count, col_count, channels = pair_repr.shape
    hidden = weight_out.shape[0]
    row_first = lax.axis_index("gx") * row_count
    col_first = lax.axis_index("gy") * col_count
    my_lengths = lax.dynamic_slice_in_dim(seq_lengths, lax.axis_index("gz") * batch_dev, batch_dev)
    row_at = row_first + jnp.arange(row_count, dtype=jnp.int32)
    col_at = col_first + jnp.arange(col_count, dtype=jnp.int32)

    def gated(normed, first, mask):
        part = weight_in[:, first : first + 2 * hidden]
        proj = jnp.einsum("ijc,cd->ijd", normed, part, preferred_element_type=jnp.float32)
        return (mask * jax.nn.sigmoid(proj[..., hidden:]) * proj[..., :hidden]).astype(
            jnp.bfloat16
        )

    masks, normed, gathered, shares = [], [], [], []
    for b in range(batch_dev):
        row_live = (row_at < my_lengths[b]).astype(jnp.float32)
        col_live = (col_at < my_lengths[b]).astype(jnp.float32)
        masks.append(row_live[:, None, None] * col_live[None, :, None])
        normed.append(layer_norm(pair_repr[b].astype(jnp.float32)).astype(jnp.bfloat16))
        left = gated(normed[b], 0, masks[b])
        gathered.append(lax.all_gather(left, "gy", axis=1, tiled=True))
    for b in range(batch_dev):
        right = gated(normed[b], 2 * hidden, masks[b])
        partial = jnp.einsum(
            "kic,kjc->ijc", gathered[b], right, preferred_element_type=jnp.float32
        ).astype(jnp.bfloat16)
        shares.append(lax.psum_scatter(partial, "gx", scatter_dimension=0, tiled=True))
    outs, total = [], jnp.float32(0)
    for b in range(batch_dev):
        gate_values = jax.nn.sigmoid(
            jnp.einsum(
                "ijc,cd->ijd", normed[b], weight_in[:, 4 * hidden :],
                preferred_element_type=jnp.float32,
            )
        )
        tri_normed = layer_norm(shares[b].astype(jnp.float32)).astype(jnp.bfloat16)
        projected = jnp.einsum(
            "ijc,cd->ijd", tri_normed, weight_out, preferred_element_type=jnp.float32
        )
        update = masks[b] * gate_values * projected
        one = (pair_repr[b].astype(jnp.float32) + update).astype(jnp.bfloat16)
        outs.append(one)
        total = total + jnp.sum(jnp.abs(one.astype(jnp.float32)))
    updated = jnp.stack(outs)
    mag_total = lax.psum(total, ("gz", "gx", "gy"))
    entry_count = (
        batch_dev
        * lax.axis_size("gz")
        * row_count
        * lax.axis_size("gx")
        * col_count
        * lax.axis_size("gy")
        * channels
    )
    magnitude = mag_total / float(entry_count)
    return (updated, magnitude)


def solution(mesh):
    return jax.shard_map(
        per_device,
        mesh=mesh,
        in_specs=(P("gz", "gx", "gy", None), P(), P(), P()),
        out_specs=(P("gz", "gx", "gy", None), P()),
        check_vma=False,
    )
```

profile of v0, /device:TPU:0, one launch (start us, length us, event | category | flops | bytes accessed | tf_op | source)
XLA Modules:
  0.0 1181.0 jit_solution(15705465478945079710)
XLA Ops:
  13.7 12.6 %fusion.38 = (f32[96,96]{1,0:T(8,128)S(1)}, f32[96,96]{1,0:T(8,128)S(1)}, f32[96,96]{1,0:T(8,128)S(1)}, f32[96,96]{1,0:T(8,128)S(1)}) fusion(f32[96,96]{1,0:T(8,128)S(1)} %get-tuple-element.33, bf16[4,96,96,128]{3,2,1,0:T(8,128)(2,1)S(1)} %copy-done.1, f32[96,96]{1,0:T(8,128)S(1)} %get-tuple-element.32, f32[96,96]{1,0:T(8,128)S(1)} %get-tuple-element.30, ...), kind=kLoop, calls=%fused_computation.59 | loop fusion | flops 18837504 | bytes 9732096 | tf_op jit(solution)/shard_map/reduce_sum | solution.py:10
  39.8 9.9 fusion.74
  52.3 6.5 fusion.105
  58.8 6.7 fusion.107
  69.9 6.5 fusion.110
  87.9 6.5 fusion.117
  94.4 6.7 fusion.115
  109.7 39.2 %all-gather.5.cloned.1.call-done = bf16[96,384,128]{2,1,0:T(8,128)(2,1)} async-done(((bf16[96,96,128]{2,1,0:T(8,128)(2,1)}), bf16[96,384,128]{2,1,0:T(8,128)(2,1)}) %all-gather.5.cloned.1.call-update) | async-done | bytes 9437200 | tf_op jit(solution)/shard_map/all_gather | solution.py:37
  148.8 13.0 %copy.63 = bf16[96,384,128]{1,0,2:T(8,128)(2,1)} copy(bf16[96,384,128]{2,1,0:T(8,128)(2,1)} %all-gather.5.cloned.1.call-done) | data formatting | bytes 18874368 | tf_op jit(solution)/shard_map/all_gather | solution.py:37
  161.9 10.2 convert_bitcast_fusion.3
  172.1 13.9 %copy.64 = bf16[384,96,128]{2,1,0:T(8,128)(2,1)} copy(bf16[384,96,128]{0,1,2:T(8,128)(2,1)} %convert_bitcast_fusion.3) | data formatting | bytes 18874368 | tf_op jit(solution)/shard_map/convert_element_type | solution.py:42
  190.3 56.6 %all-gather.7.cloned.1.call-done = bf16[96,384,128]{2,1,0:T(8,128)(2,1)} async-done(((bf16[96,96,128]{2,1,0:T(8,128)(2,1)}), bf16[96,384,128]{2,1,0:T(8,128)(2,1)}) %all-gather.7.cloned.1.call-update) | async-done | bytes 9437200 | tf_op jit(solution)/shard_map/all_gather | solution.py:37
  246.9 13.0 %copy.70 = bf16[96,384,128]{1,0,2:T(8,128)(2,1)} copy(bf16[96,384,128]{2,1,0:T(8,128)(2,1)} %all-gather.7.cloned.1.call-done) | data formatting | bytes 18874368 | tf_op jit(solution)/shard_map/all_gather | solution.py:37
  259.9 10.2 convert_bitcast_fusion.2
  270.2 13.9 %copy.71 = bf16[384,96,128]{2,1,0:T(8,128)(2,1)} copy(bf16[384,96,128]{0,1,2:T(8,128)(2,1)} %convert_bitcast_fusion.2) | data formatting | bytes 18874368 | tf_op jit(solution)/shard_map/convert_element_type | solution.py:42
  288.3 56.7 %all-gather.9.cloned.1.call-done = bf16[96,384,128]{2,1,0:T(8,128)(2,1)} async-done(((bf16[96,96,128]{2,1,0:T(8,128)(2,1)}), bf16[96,384,128]{2,1,0:T(8,128)(2,1)}) %all-gather.9.cloned.1.call-update) | async-done | bytes 9437200 | tf_op jit(solution)/shard_map/all_gather | solution.py:37
  345.0 13.1 %copy.77 = bf16[96,384,128]{1,0,2:T(8,128)(2,1)} copy(bf16[96,384,128]{2,1,0:T(8,128)(2,1)} %all-gather.9.cloned.1.call-done) | data formatting | bytes 18874368 | tf_op jit(solution)/shard_map/all_gather | solution.py:37
  358.0 10.2 convert_bitcast_fusion.1
  368.2 14.0 %copy.78 = bf16[384,96,128]{2,1,0:T(8,128)(2,1)} copy(bf16[384,96,128]{0,1,2:T(8,128)(2,1)} %convert_bitcast_fusion.1) | data formatting | bytes 18874368 | tf_op jit(solution)/shard_map/convert_element_type | solution.py:42
  386.7 56.2 %all-gather.11.cloned.1.call-done = bf16[96,384,128]{2,1,0:T(8,128)(2,1)} async-done(((bf16[96,96,128]{2,1,0:T(8,128)(2,1)}), bf16[96,384,128]{2,1,0:T(8,128)(2,1)}) %all-gather.11.cloned.1.call-update) | async-done | bytes 9437200 | tf_op jit(solution)/shard_map/all_gather | solution.py:37
  442.9 13.0 %copy.84 = bf16[96,384,128]{1,0,2:T(8,128)(2,1)} copy(bf16[96,384,128]{2,1,0:T(8,128)(2,1)} %all-gather.11.cloned.1.call-done) | data formatting | bytes 18874368 | tf_op jit(solution)/shard_map/all_gather | solution.py:37
  455.9 9.9 convert_bitcast_fusion
  465.8 13.8 %copy.85 = bf16[384,96,128]{2,1,0:T(8,128)(2,1)} copy(bf16[384,96,128]{0,1,2:T(8,128)(2,1)} %convert_bitcast_fusion) | data formatting | bytes 18874368 | tf_op jit(solution)/shard_map/convert_element_type | solution.py:42
  479.6 126.7 %reduce-scatter.5.cloned.1.call-done = bf16[96,96,128]{2,1,0:T(8,128)(2,1)} async-done(((bf16[384,96,128]{2,1,0:T(8,128)(2,1)}), bf16[96,96,128]{2,1,0:T(8,128)(2,1)}) %reduce-scatter.5.cloned.1.call-update) | async-done | bytes 2359312 | tf_op jit(solution)/shard_map/reduce_scatter | solution.py:43
  614.0 156.7 %reduce-scatter.7.cloned.1.call-done = bf16[96,96,128]{2,1,0:T(8,128)(2,1)} async-done(((bf16[384,96,128]{2,1,0:T(8,128)(2,1)}), bf16[96,96,128]{2,1,0:T(8,128)(2,1)}) %reduce-scatter.7.cloned.1.call-update) | async-done | bytes 2359312 | tf_op jit(solution)/shard_map/reduce_scatter | solution.py:43
  779.0 156.3 %reduce-scatter.9.cloned.1.call-done = bf16[96,96,128]{2,1,0:T(8,128)(2,1)} async-done(((bf16[384,96,128]{2,1,0:T(8,128)(2,1)}), bf16[96,96,128]{2,1,0:T(8,128)(2,1)}) %reduce-scatter.9.cloned.1.call-update) | async-done | bytes 2359312 | tf_op jit(solution)/shard_map/reduce_scatter | solution.py:43
  961.1 7.8 abs_reduce_fusion.2
  968.9 8.2 abs_reduce_fusion.1
  977.1 123.2 %reduce-scatter.11.cloned.1.call-done = bf16[96,96,128]{2,1,0:T(8,128)(2,1)} async-done(((bf16[384,96,128]{2,1,0:T(8,128)(2,1)}), bf16[96,96,128]{2,1,0:T(8,128)(2,1)}) %reduce-scatter.11.cloned.1.call-update) | async-done | bytes 2359312 | tf_op jit(solution)/shard_map/reduce_scatter | solution.py:43
  1111.8 8.2 abs_reduce_fusion
  1122.5 41.2 %psum.7 = f32[]{:T(128)} all-reduce(f32[]{:T(128)S(6)} %add.203), channel_id=1, replica_groups=mesh['gz'=2,'gx'=4,'gy'=4] {'gz','gx','gy'}, use_global_device_ids=true, to_apply=%region_24.0 | all-reduce | flops 1 | bytes 8 | tf_op jit(solution)/shard_map/psum | solution.py:61
  1164.3 8.2 pad_maximum_fusion
  (141 shorter events, 112.3 us)
Async XLA Ops:
  7.2 935.3 %copy-start = (bf16[128,128]{1,0:T(8,128)(2,1)S(1)}, bf16[128,128]{1,0:T(8,128)(2,1)}, u32[]{:S(2)}) copy-start(bf16[128,128]{1,0:T(8,128)(2,1)} %param.7) | copy-start | bytes 98308
  7.2 141.6 %all-gather.5.cloned.1.call-start = ((), (), s32[]{:S(2)}) async-start(), calls=%async_computation.4 | async-start | bytes 11796480 | tf_op jit(solution)/shard_map/all_gather | solution.py:37
  13.4 18.8 %copy-start.10 = (f32[96,96]{1,0:T(8,128)}, f32[96,96]{1,0:T(8,128)S(1)}, u32[]{:S(2)}) copy-start(f32[96,96]{1,0:T(8,128)S(1)} %get-tuple-element.33) | copy-start | bytes 110596
  13.4 45.4 %copy-start.8 = (f32[96,96]{1,0:T(8,128)}, f32[96,96]{1,0:T(8,128)S(1)}, u32[]{:S(2)}) copy-start(f32[96,96]{1,0:T(8,128)S(1)} %get-tuple-element.32) | copy-start | bytes 110596
  13.7 12.6 %copy-start.6 = (bf16[128,640]{1,0:T(8,128)(2,1)S(1)}, bf16[128,640]{1,0:T(8,128)(2,1)}, u32[]{:S(2)}) copy-start(bf16[128,640]{1,0:T(8,128)(2,1)} %param.6) | copy-start | bytes 491524
  39.8 9.9 copy-start.24
  49.7 197.2 %all-gather.7.cloned.1.call-start = ((), (), s32[]{:S(2)}) async-start(), calls=%async_computation.6 | async-start | bytes 11796480 | tf_op jit(solution)/shard_map/all_gather | solution.py:37
  52.2 13.3 %copy-start.26 = (f32[96,96]{1,0:T(8,128)}, f32[96,96]{1,0:T(8,128)S(1)}, u32[]{:S(2)}) copy-start(f32[96,96]{1,0:T(8,128)S(1)} %broadcast_multiply_fusion.2) | copy-start | bytes 110596
  52.3 6.6 copy-start.14
  69.7 275.2 %all-gather.9.cloned.1.call-start = ((), (), s32[]{:S(2)}) async-start(), calls=%async_computation.8 | async-start | bytes 11796480 | tf_op jit(solution)/shard_map/all_gather | solution.py:37
  69.9 13.1 %copy-start.28 = (f32[96,96]{1,0:T(8,128)}, f32[96,96]{1,0:T(8,128)S(1)}, u32[]{:S(2)}) copy-start(f32[96,96]{1,0:T(8,128)S(1)} %broadcast_multiply_fusion.1) | copy-start | bytes 110596
  69.9 6.5 copy-start.16
  87.1 355.8 %all-gather.11.cloned.1.call-start = ((), (), s32[]{:S(2)}) async-start(), calls=%async_computation.10 | async-start | bytes 11796480 | tf_op jit(solution)/shard_map/all_gather | solution.py:37
  87.8 13.3 %copy-start.30 = (f32[96,96]{1,0:T(8,128)}, f32[96,96]{1,0:T(8,128)S(1)}, u32[]{:S(2)}) copy-start(f32[96,96]{1,0:T(8,128)S(1)} %broadcast_multiply_fusion) | copy-start | bytes 110596
  105.2 501.1 %reduce-scatter.5.cloned.1.call-start = ((), (), s32[]{:S(2)}) async-start(), calls=%async_computation.5 | async-start | bytes 11796480 | tf_op jit(solution)/shard_map/reduce_scatter | solution.py:43
  186.1 584.7 %reduce-scatter.7.cloned.1.call-start = ((), (), s32[]{:S(2)}) async-start(), calls=%async_computation.7 | async-start | bytes 11796480 | tf_op jit(solution)/shard_map/reduce_scatter | solution.py:43
  284.1 651.2 %reduce-scatter.9.cloned.1.call-start = ((), (), s32[]{:S(2)}) async-start(), calls=%async_computation.9 | async-start | bytes 11796480 | tf_op jit(solution)/shard_map/reduce_scatter | solution.py:43
  382.3 718.1 %reduce-scatter.11.cloned.1.call-start = ((), (), s32[]{:S(2)}) async-start(), calls=%async_computation.11 | async-start | bytes 11796480 | tf_op jit(solution)/shard_map/reduce_scatter | solution.py:43
  614.0 328.5 %copy-start.2 = (bf16[96,96,128]{2,1,0:T(8,128)(2,1)S(1)}, bf16[96,96,128]{2,1,0:T(8,128)(2,1)}, u32[]{:S(2)}) copy-start(bf16[96,96,128]{2,1,0:T(8,128)(2,1)} %reduce-scatter.5.cloned.1.call-done) | copy-start | bytes 7077892
  773.9 181.3 %slice-start = ((s8[9437184]{0:T(1024)(128)(4,1)}), s8[1048576]{0:T(1024)(128)(4,1)S(1)}, s32[]{:S(2)}) async-start(s8[9437184]{0:T(1024)(128)(4,1)} %bitcast.152), calls=%async_computation.12 | async-start | bytes 2097152
  935.3 7.2 copy-start.21
  935.3 7.2 copy-start.32
  937.9 8.8 copy-start.3
  937.9 8.8 copy-start.23
  937.9 8.8 copy-start.33
  942.5 12.7 %slice-start.1 = ((s8[9437184]{0:T(1024)(128)(4,1)}), s8[4194304]{0:T(1024)(128)(4,1)S(1)}, s32[]{:S(2)}) async-start(s8[9437184]{0:T(1024)(128)(4,1)} %bitcast.152), calls=%async_computation.13 | async-start | bytes 8388608
  946.7 8.5 slice-start.2
  961.1 7.8 copy-start.17
  961.1 7.8 copy-start.29
  1100.4 7.2 copy-start.4
  1103.1 8.6 copy-start.19
  1103.1 8.6 copy-start.31
  (14 other events, 68.8 us)
Sparse Core Ops, SparseCore 0:
  49.8 98.9 all-gather.4
  150.7 96.1 all-gather.6
  248.7 96.1 all-gather.8
  346.7 96.1 all-gather.10
  445.1 161.1 reduce-scatter.4
  608.6 162.1 reduce-scatter.6
  773.1 162.1 reduce-scatter.8
  938.2 162.1 reduce-scatter.10
where the time goes:
time: 1190 us; the launch traced here: 1180 us
  waiting for transfers between devices  772 us (65%)
  matrix products  139 us (12%)
  local copies, waits for them, and re-layouts  126 us (11%)
  other arithmetic  82.6 us (7%)
  blocking collectives  41.2 us (3%)
  between operations  19.6 us (2%)
    reduce_scatter x4, waiting for transfers between devices, per_device(): lax.psum_scatter(partial, 'gx', scatter_dimension=0, tiled=True)  563 us
    all_gather x4, waiting for transfers between devices, per_device(): gathered.append(lax.all_gather(left, 'gy', axis=1, tiled=True))  209 us
    convert_element_type x4, local copies, waits for them, and re-layouts, per_device(): partial = jnp.einsum('kic,kjc->ijc', gathered[b], right, preferred_elemen...  55.6 us
    all_gather x4, local copies, waits for them, and re-layouts, per_device(): gathered.append(lax.all_gather(left, 'gy', axis=1, tiled=True))  52.1 us
    dot_general x8, matrix products, gated(): jnp.einsum('ijc,cd->ijd', normed, part, preferred_element_type=jnp.float32)  51.6 us
    psum x1, blocking collectives, per_device(): mag_total = lax.psum(total, ('gz', 'gx', 'gy'))  41.2 us
    dot_general x4, matrix products, per_device(): jnp.einsum('kic,kjc->ijc', gathered[b], right, preferred_element_type=jnp...  40.6 us
    reduce_sum x5, other arithmetic, layer_norm(): variance = jnp.mean(centered * centered, axis=-1, keepdims=True)  30.3 us
  transfers between devices with their start and end apart: 8, of which 8 were waited for; matrix products, arithmetic and copies ran while one was open for 23% of the time, Pallas kernels for 0%

commit v1 on v0

--- a/solution.py
+++ b/solution.py
@@ -2,6 +2,8 @@
 import jax.numpy as jnp
 from jax import lax
 from jax.sharding import PartitionSpec as P
+
+CHUNKS = 3
 
 
 def layer_norm(values):
@@ -11,7 +13,82 @@
     return centered * lax.rsqrt(variance + 1e-05)
 
 
-def per_device(pair_repr, seq_lengths, weight_in, weight_out):
+def project(normed, weight):
+    return jnp.einsum("ijc,cd->ijd", normed, weight, preferred_element_type=jnp.float32)
+
+
+def rehomed(pair_repr, seq_lengths, weight_in, weight_out):
+    batch_dev, row_count, col_count, channels = pair_repr.shape
+    hidden = weight_out.shape[0]
+    ring = batch_dev
+    me = lax.axis_index("gx")
+    row_first = me * row_count
+    col_first = lax.axis_index("gy") * col_count
+    my_lengths = lax.dynamic_slice_in_dim(seq_lengths, lax.axis_index("gz") * batch_dev, batch_dev)
+    my_length = lax.dynamic_index_in_dim(my_lengths, me, 0, keepdims=False)
+    col_at = col_first + jnp.arange(col_count, dtype=jnp.int32)
+    row_local = jnp.arange(row_count, dtype=jnp.int32)
+    width = col_count // CHUNKS
+    tall = row_count // CHUNKS
+
+    def shift(value, step):
+        if step == 0:
+            return value
+        return lax.ppermute(value, "gx", [(i, (i + step) % ring) for i in range(ring)])
+
+    def gated(normed, first, mask):
+        proj = project(normed, weight_in[:, first : first + 2 * hidden])
+        return (mask * jax.nn.sigmoid(proj[..., hidden:]) * proj[..., :hidden]).astype(
+            jnp.bfloat16
+        )
+
+    to = [lax.rem(me + s, ring) for s in range(ring)]
+    source = [lax.rem(me + ring - s, ring) for s in range(ring)]
+    outgoing = [lax.dynamic_index_in_dim(pair_repr, to[s], 0, keepdims=False) for s in range(ring)]
+    k_at = jnp.concatenate([source[s] * row_count + row_local for s in range(ring)])
+    k_live = (k_at < my_length).astype(jnp.float32)
+
+    lefts, rights = [], []
+    for t in range(CHUNKS):
+        cols = slice(t * width, (t + 1) * width)
+        got = [shift(outgoing[s][:, cols], s) for s in range(ring)]
+        mine = jnp.concatenate(got, axis=0)
+        normed = layer_norm(mine.astype(jnp.float32)).astype(jnp.bfloat16)
+        live = (col_at[cols] < my_length).astype(jnp.float32)
+        mask = k_live[:, None, None] * live[None, :, None]
+        left = gated(normed, 0, mask)
+        lefts.append(lax.all_gather(left, "gy", axis=0))
+        rights.append(gated(normed, 2 * hidden, mask))
+    right = jnp.concatenate(rights, axis=1)
+
+    updated = jnp.zeros_like(pair_repr)
+    total = jnp.float32(0)
+    for t in range(CHUNKS):
+        rows = slice(t * tall, (t + 1) * tall)
+        triangle = jnp.einsum("gkic,kjc->gijc", lefts[t], right, preferred_element_type=jnp.float32)
+        tri_normed = layer_norm(triangle).astype(jnp.bfloat16)
+        for s in range(ring):
+            home = shift(lax.dynamic_index_in_dim(tri_normed, to[s], 0, keepdims=False), s)
+            b = source[s]
+            own = lax.dynamic_slice(
+                pair_repr, (b, t * tall, 0, 0), (1, tall, col_count, channels)
+            )[0].astype(jnp.float32)
+            length = lax.dynamic_index_in_dim(my_lengths, b, 0, keepdims=False)
+            row_live = (row_first + row_local[rows] < length).astype(jnp.float32)
+            col_live = (col_at < length).astype(jnp.float32)
+            mask = row_live[:, None, None] * col_live[None, :, None]
+            gate_values = jax.nn.sigmoid(
+                project(layer_norm(own).astype(jnp.bfloat16), weight_in[:, 4 * hidden :])
+            )
+            one = (own + mask * gate_values * project(home, weight_out)).astype(jnp.bfloat16)
+            updated = lax.dynamic_update_slice(updated, one[None], (b, t * tall, 0, 0))
+            total = total + jnp.sum(jnp.abs(one.astype(jnp.float32)))
+    mag_total = lax.psum(total, ("gz", "gx", "gy"))
+    entry_count = batch_dev * lax.axis_size("gz") * row_count * ring * col_count * lax.axis_size("gy") * channels
+    return (updated, mag_total / float(entry_count))
+
+
+def gathered_columns(pair_repr, seq_lengths, weight_in, weight_out):
     batch_dev, row_count, col_count, channels = pair_repr.shape
     hidden = weight_out.shape[0]
     row_first = lax.axis_index("gx") * row_count
@@ -72,6 +149,14 @@
     return (updated, magnitude)
 
 
+def per_device(pair_repr, seq_lengths, weight_in, weight_out):
+    batch_dev, row_count, col_count, _ = pair_repr.shape
+    fits = row_count % CHUNKS == 0 and col_count % CHUNKS == 0
+    if fits and lax.axis_size("gx") == batch_dev and lax.axis_size("gy") == batch_dev:
+        return rehomed(pair_repr, seq_lengths, weight_in, weight_out)
+    return gathered_columns(pair_repr, seq_lengths, weight_in, weight_out)
+
+
 def solution(mesh):
     return jax.shard_map(
         per_device,

time: 1190 us -> 758 us (0.64)
  waiting for transfers between devices: 772 us -> 187 us
  other arithmetic: 82.6 us -> 179 us
  starting transfers between devices: 0.72 us -> 75.6 us
  matrix products: 139 us -> 118 us
  blocking collectives: 41.2 us -> 53.3 us
    reduce_scatter x4 -> x0, waiting for transfers between devices: 563 us -> none  [per_device(): lax.psum_scatter(partial, 'gx', scatter_dimension=0, tiled=True)]
    all_gather x4 -> x3, waiting for transfers between devices: 209 us -> 0.01 us  [rehomed(): lefts.append(lax.all_gather(left, 'gy', axis=0))]
    ppermute x0 -> x18, waiting for transfers between devices: none -> 187 us  [shift(): lax.ppermute(value, 'gx', [(i, (i + step) % ring) for i in range(ring)])]
    ppermute x0 -> x18, starting transfers between devices: none -> 75.5 us  [shift(): lax.ppermute(value, 'gx', [(i, (i + step) % ring) for i in range(ring)])]
    convert_element_type x8 -> x0, local copies, waits for them, and re-layouts: 72.3 us -> none  [the longest x4 55.6 us: per_device(): partial = jnp.einsum('kic,kjc->ijc', gathered[b], right, preferred_elemen...]
    convert_element_type x4 -> x15, other arithmetic: 3.59 us -> 53.9 us  [the longest x3 36.3 us: rehomed(): normed = layer_norm(mine.astype(jnp.float32)).astype(jnp.bfloat16)]
    reduce_sum x5 -> x7, other arithmetic: 30.3 us -> 65.9 us  [layer_norm(): variance = jnp.mean(centered * centered, axis=-1, keepdims=True)]
    dynamic_slice x1 -> x15, local copies, waits for them, and re-layouts: 0.07 us -> 30.7 us  [the longest x14 30 us: rehomed(): lax.dynamic_index_in_dim(tri_normed, to[s], 0, keepdims=False)]
  transfers between devices with their start and end apart: 8 -> 21, of which waited for: 8 -> 8; matrix products, arithmetic and copies ran while one was open for 23% -> 48% of each run, Pallas kernels for 0% -> 0%
where the time goes in v1:
time: 758 us; the launch traced here: 752 us
  waiting for transfers between devices  187 us (25%)
  other arithmetic  179 us (24%)
  matrix products  118 us (16%)
  local copies, waits for them, and re-layouts  115 us (15%)
  starting transfers between devices  75.6 us (10%)
  blocking collectives  53.3 us (7%)
  between operations  24.2 us (3%)
    ppermute x18, waiting for transfers between devices, shift(): lax.ppermute(value, 'gx', [(i, (i + step) % ring) for i in range(ring)])  187 us
    ppermute x18, starting transfers between devices, shift(): lax.ppermute(value, 'gx', [(i, (i + step) % ring) for i in range(ring)])  75.5 us
    dot_general x30, matrix products, project(): jnp.einsum('ijc,cd->ijd', normed, weight, preferred_element_type=jnp.floa...  68.7 us
    reduce_sum x7, other arithmetic, layer_norm(): variance = jnp.mean(centered * centered, axis=-1, keepdims=True)  65.9 us
    psum x1, blocking collectives, rehomed(): mag_total = lax.psum(total, ('gz', 'gx', 'gy'))  53.3 us
    all_gather x3, local copies, waits for them, and re-layouts, rehomed(): lefts.append(lax.all_gather(left, 'gy', axis=0))  50.5 us
    dot_general x3, matrix products, rehomed(): jnp.einsum('gkic,kjc->gijc', lefts[t], right, preferred_element_type=jnp....  49.5 us
    convert_element_type x3, other arithmetic, rehomed(): normed = layer_norm(mine.astype(jnp.float32)).astype(jnp.bfloat16)  36.3 us
  transfers between devices with their start and end apart: 21, of which 8 were waited for; matrix products, arithmetic and copies ran while one was open for 48% of the time, Pallas kernels for 0%

profile of v1, /device:TPU:0, one launch (start us, length us, event | category | flops | bytes accessed | tf_op | source)
XLA Modules:
  0.0 752.3 jit_solution(6077061796652901205)
XLA Ops:
  7.3 5.6 dynamic-slice_bitcast_fusion.3
  28.4 9.8 %collective-permute-done = bf16[96,32,128]{2,1,0:T(8,128)(2,1)S(1)} collective-permute-done((bf16[96,32,128]{2,1,0:T(8,128)(2,1)}, bf16[96,32,128]{2,1,0:T(8,128)(2,1)S(1)}, u32[]{:S(2)}, u32[]{:S(2)}) %collective-permute-start) | collective-permute-done | bytes 786464 | tf_op jit(solution)/shard_map/ppermute | solution.py:37
  38.1 33.0 %collective-permute-done.1 = bf16[96,32,128]{2,1,0:T(8,128)(2,1)} collective-permute-done((bf16[96,32,128]{2,1,0:T(8,128)(2,1)}, bf16[96,32,128]{2,1,0:T(8,128)(2,1)}, u32[]{:S(2)}, u32[]{:S(2)}) %collective-permute-start.1) | collective-permute-done | bytes 786464 | tf_op jit(solution)/shard_map/ppermute | solution.py:37
  74.6 13.2 %fusion.10 = f32[384,32]{1,0:T(8,128)S(1)} fusion(f32[384,32]{1,0:T(8,128)S(1)} %broadcast_multiply_fusion.2, bf16[96,32,128]{2,1,0:T(8,128)(2,1)} %collective-permute-done.2, bf16[96,32,128]{2,1,0:T(8,128)(2,1)} %collective-permute-done.1, bf16[96,32,128]{2,1,0:T(8,128)(2,1)S(1)} %collective-permute-done, bf16[96,32,128]{2,1,0:T(8,128)(2,1)S(1)} %get-tuple-element.48), kind=kLoop, calls=%fused_computation.29 | loop fusion | flops 10997760 | bytes 3244032 | tf_op jit(solution)/shard_map/reduce_sum | solution.py:12
  87.8 10.7 %fusion.11 = bf16[384,32,128]{2,1,0:T(8,128)(2,1)S(1)} fusion(f32[384,32]{1,0:T(8,128)S(1)} %add_rsqrt_fusion.2, f32[384,32]{1,0:T(8,128)S(1)} %broadcast_multiply_fusion.2, bf16[96,32,128]{2,1,0:T(8,128)(2,1)} %collective-permute-done.2, bf16[96,32,128]{2,1,0:T(8,128)(2,1)} %collective-permute-done.1, bf16[96,32,128]{2,1,0:T(8,128)(2,1)S(1)} %collective-permute-done, ...), kind=kLoop, calls=%fused_computation.30 | loop fusion | flops 11010048 | bytes 6389760 | tf_op jit(solution)/shard_map/convert_element_type | solution.py:56
  107.8 17.4 %collective-permute-start.3 = (bf16[96,32,128]{2,1,0:T(8,128)(2,1)}, bf16[96,32,128]{2,1,0:T(8,128)(2,1)S(1)}, u32[]{:S(2)}, u32[]{:S(2)}) collective-permute-start(bf16[96,32,128]{2,1,0:T(8,128)(2,1)} %get-tuple-element.53), channel_id=1, source_target_pairs={{0,4},{4,8},{8,12},{12,0},{1,5},{5,9},{9,13},{13,1},{2,6},{6,10},{... | collective-permute-start | bytes 2359304 | tf_op jit(solution)/shard_map/ppermute | solution.py:37
  128.0 17.0 %collective-permute-done.3 = bf16[96,32,128]{2,1,0:T(8,128)(2,1)S(1)} collective-permute-done((bf16[96,32,128]{2,1,0:T(8,128)(2,1)}, bf16[96,32,128]{2,1,0:T(8,128)(2,1)S(1)}, u32[]{:S(2)}, u32[]{:S(2)}) %collective-permute-start.3) | collective-permute-done | bytes 786464 | tf_op jit(solution)/shard_map/ppermute | solution.py:37
  144.9 32.0 %collective-permute-done.4 = bf16[96,32,128]{2,1,0:T(8,128)(2,1)S(1)} collective-permute-done((bf16[96,32,128]{2,1,0:T(8,128)(2,1)}, bf16[96,32,128]{2,1,0:T(8,128)(2,1)S(1)}, u32[]{:S(2)}, u32[]{:S(2)}) %collective-permute-start.4) | collective-permute-done | bytes 786464 | tf_op jit(solution)/shard_map/ppermute | solution.py:37
  176.9 6.2 convert_reduce_fusion.1
  183.1 10.7 %fusion.8 = f32[384,32]{1,0:T(8,128)S(1)} fusion(f32[384,32]{1,0:T(8,128)S(1)} %broadcast_multiply_fusion.1, bf16[96,32,128]{2,1,0:T(8,128)(2,1)S(1)} %collective-permute-done.5, bf16[96,32,128]{2,1,0:T(8,128)(2,1)S(1)} %collective-permute-done.4, bf16[96,32,128]{2,1,0:T(8,128)(2,1)S(1)} %collective-permute-done.3, bf16[96,32,128]{2,1,0:T(8,128)(2,1)S(1)} %copy-done.8), kind=kLoop, calls=%fused_computation.27 | loop fusion | flops 10997760 | bytes 3244032 | tf_op jit(solution)/shard_map/reduce_sum | solution.py:12
  193.8 17.8 %fusion.9 = bf16[384,32,128]{2,1,0:T(8,128)(2,1)S(1)} fusion(f32[384,32]{1,0:T(8,128)S(1)} %add_rsqrt_fusion.1, f32[384,32]{1,0:T(8,128)S(1)} %broadcast_multiply_fusion.1, bf16[96,32,128]{2,1,0:T(8,128)(2,1)S(1)} %collective-permute-done.5, bf16[96,32,128]{2,1,0:T(8,128)(2,1)S(1)} %collective-permute-done.4, ...), kind=kLoop, calls=%fused_computation.28 | loop fusion | flops 11010048 | bytes 6389760 | tf_op jit(solution)/shard_map/convert_element_type | solution.py:56
  216.0 5.5 fusion.17
  221.5 17.3 %collective-permute-start.6 = (bf16[96,32,128]{2,1,0:T(8,128)(2,1)}, bf16[96,32,128]{2,1,0:T(8,128)(2,1)}, u32[]{:S(2)}, u32[]{:S(2)}) collective-permute-start(bf16[96,32,128]{2,1,0:T(8,128)(2,1)} %get-tuple-element.52), channel_id=1, source_target_pairs={{0,4},{4,8},{8,12},{12,0},{1,5},{5,9},{9,13},{13,1},{2,6},{6,10},{... | collective-permute-start | bytes 2359304 | tf_op jit(solution)/shard_map/ppermute | solution.py:37
  244.5 15.0 %collective-permute-done.6 = bf16[96,32,128]{2,1,0:T(8,128)(2,1)} collective-permute-done((bf16[96,32,128]{2,1,0:T(8,128)(2,1)}, bf16[96,32,128]{2,1,0:T(8,128)(2,1)}, u32[]{:S(2)}, u32[]{:S(2)}) %collective-permute-start.6) | collective-permute-done | bytes 786464 | tf_op jit(solution)/shard_map/ppermute | solution.py:37
  259.5 32.5 %collective-permute-done.7 = bf16[96,32,128]{2,1,0:T(8,128)(2,1)} collective-permute-done((bf16[96,32,128]{2,1,0:T(8,128)(2,1)}, bf16[96,32,128]{2,1,0:T(8,128)(2,1)}, u32[]{:S(2)}, u32[]{:S(2)}) %collective-permute-start.7) | collective-permute-done | bytes 786464 | tf_op jit(solution)/shard_map/ppermute | solution.py:37
  295.5 12.2 %fusion.6 = f32[384,32]{1,0:T(8,128)S(1)} fusion(f32[384,32]{1,0:T(8,128)S(1)} %broadcast_multiply_fusion, bf16[96,32,128]{2,1,0:T(8,128)(2,1)} %collective-permute-done.8, bf16[96,32,128]{2,1,0:T(8,128)(2,1)} %collective-permute-done.7, bf16[96,32,128]{2,1,0:T(8,128)(2,1)} %collective-permute-done.6, bf16[96,32,128]{2,1,0:T(8,128)(2,1)S(1)} %copy-done.7), kind=kLoop, calls=%fused_computation.25 | loop fusion | flops 10997760 | bytes 3244032 | tf_op jit(solution)/shard_map/reduce_sum | solution.py:12
  307.7 7.8 %fusion.7 = bf16[384,32,128]{2,1,0:T(8,128)(2,1)S(1)} fusion(f32[384,32]{1,0:T(8,128)S(1)} %add_rsqrt_fusion, f32[384,32]{1,0:T(8,128)S(1)} %broadcast_multiply_fusion, bf16[96,32,128]{2,1,0:T(8,128)(2,1)} %collective-permute-done.8, bf16[96,32,128]{2,1,0:T(8,128)(2,1)} %collective-permute-done.7, bf16[96,32,128]{2,1,0:T(8,128)(2,1)} %collective-permute-done.6, ...), kind=kLoop, calls=%fused_computation.26 | loop fusion | flops 11010048 | bytes 6389760 | tf_op jit(solution)/shard_map/convert_element_type | solution.py:56
  319.9 5.4 fusion.12
  332.4 7.3 convert_reduce_fusion.3
  340.0 15.8 %fusion.102 = (f32[32,96]{1,0:T(8,128)S(1)}, f32[32,96]{1,0:T(8,128)S(1)}, f32[32,96]{1,0:T(8,128)S(1)}, f32[32,96]{1,0:T(8,128)S(1)}, f32[32,96]{1,0:T(8,128)S(...) fusion(f32[32,96]{1,0:T(8,128)S(1)} %broadcast_multiply_fusion., ...), kind=kLoop, calls=%fused_computation.164 | loop fusion | flops 18837504 | bytes 9732112 | tf_op jit(solution)/shard_map/reduce_sum | solution.py:12
  383.5 13.2 %copy.36 = bf16[384,96,128,1]{0,1,3,2:T(8,128)(2,1)} copy(bf16[384,96,128,1]{2,0,1,3:T(8,128)(2,1)} %maximum_bitcast_fusion) | data formatting | bytes 18874368 | tf_op jit(solution)/shard_map/concatenate | solution.py:62
  396.7 16.8 %copy.17 = bf16[4,384,32,128]{1,2,0,3:T(8,128)(2,1)} copy(bf16[4,384,32,128]{3,1,0,2:T(8,128)(2,1)} %bitcast.400) | data formatting | bytes 25165824 | tf_op jit(solution)/shard_map/all_gather | solution.py:60
  413.5 16.5 %bitcast_reduce_fusion.2 = (f32[4,32,96]{2,1,0:T(8,128)S(1)}, f32[128,96,4,32]{1,3,2,0:T(8,128)}) fusion(bf16[384,96,128,1]{0,1,3,2:T(8,128)(2,1)} %copy.36, bf16[4,384,32,128]{1,2,0,3:T(8,128)(2,1)} %copy.17), kind=kOutput, calls=%fused_computation.6 | convolution fusion | flops 1209520128 | bytes 28360704 | tf_op jit(solution)/shard_map/gkic,kjc->gijc/dot_general | solution.py:68
  443.3 16.5 %collective-permute-start.9 = (bf16[32,96,128]{2,1,0:T(8,128)(2,1)}, bf16[32,96,128]{2,1,0:T(8,128)(2,1)}, u32[]{:S(2)}, u32[]{:S(2)}) collective-permute-start(bf16[32,96,128]{2,1,0:T(8,128)(2,1)} %bitcast.407), channel_id=1, source_target_pairs={{0,4},{4,8},{8,12},{12,0},{1,5},{5,9},{9,13},{13,1},{2,6},{6,10},{... | collective-permute-start | bytes 2359304 | tf_op jit(solution)/shard_map/ppermute | solution.py:37
  465.9 16.9 %copy.24 = bf16[4,384,32,128]{1,2,0,3:T(8,128)(2,1)} copy(bf16[4,384,32,128]{3,1,0,2:T(8,128)(2,1)} %bitcast.401) | data formatting | bytes 25165824 | tf_op jit(solution)/shard_map/all_gather | solution.py:60
  482.8 16.4 %bitcast_reduce_fusion.1 = (f32[4,32,96]{2,1,0:T(8,128)S(1)}, f32[128,96,4,32]{1,3,2,0:T(8,128)}) fusion(bf16[384,96,128,1]{0,1,3,2:T(8,128)(2,1)} %copy.36, bf16[4,384,32,128]{1,2,0,3:T(8,128)(2,1)} %copy.24), kind=kOutput, calls=%fused_computation.4 | convolution fusion | flops 1209520128 | bytes 28360704 | tf_op jit(solution)/shard_map/gkic,kjc->gijc/dot_general | solution.py:68
  508.2 16.8 %copy.31 = bf16[4,384,32,128]{1,2,0,3:T(8,128)(2,1)} copy(bf16[4,384,32,128]{3,1,0,2:T(8,128)(2,1)} %bitcast.402) | data formatting | bytes 25165824 | tf_op jit(solution)/shard_map/all_gather | solution.py:60
  525.0 16.6 %bitcast_reduce_fusion = (f32[4,32,96]{2,1,0:T(8,128)S(1)}, f32[128,96,4,32]{1,3,2,0:T(8,128)}) fusion(bf16[384,96,128,1]{0,1,3,2:T(8,128)(2,1)} %copy.36, bf16[4,384,32,128]{1,2,0,3:T(8,128)(2,1)} %copy.31), kind=kOutput, calls=%fused_computation.2 | convolution fusion | flops 1209520128 | bytes 28360704 | tf_op jit(solution)/shard_map/gkic,kjc->gijc/dot_general | solution.py:68
  562.0 5.2 broadcast_in_dim.26
  618.4 25.1 %collective-permute-done.14 = bf16[32,96,128]{2,1,0:T(8,128)(2,1)S(1)} collective-permute-done((bf16[32,96,128]{2,1,0:T(8,128)(2,1)}, bf16[32,96,128]{2,1,0:T(8,128)(2,1)S(1)}, u32[]{:S(2)}, u32[]{:S(2)}) %collective-permute-start.14) | collective-permute-done | bytes 786464 | tf_op jit(solution)/shard_map/ppermute | solution.py:37
  654.7 22.9 %collective-permute-done.16 = bf16[32,96,128]{2,1,0:T(8,128)(2,1)S(1)} collective-permute-done((bf16[32,96,128]{2,1,0:T(8,128)(2,1)S(1)}, bf16[32,96,128]{2,1,0:T(8,128)(2,1)S(1)}, u32[]{:S(2)}, u32[]{:S(2)}) %collective-permute-start.16) | collective-permute-done | bytes 786464 | tf_op jit(solution)/shard_map/ppermute | solution.py:37
  690.4 53.3 %psum.7 = f32[]{:T(128)} all-reduce(f32[]{:T(128)S(6)} %add.523), channel_id=1, replica_groups=mesh['gz'=2,'gx'=4,'gy'=4] {'gz','gx','gy'}, use_global_device_ids=true, to_apply=%region_48.49 | all-reduce | flops 1 | bytes 8 | tf_op jit(solution)/shard_map/psum | solution.py:86
  (233 shorter events, 200.1 us)
Async XLA Ops:
  7.2 553.4 %copy-start = (bf16[128,128]{1,0:T(8,128)(2,1)S(1)}, bf16[128,128]{1,0:T(8,128)(2,1)}, u32[]{:S(2)}) copy-start(bf16[128,128]{1,0:T(8,128)(2,1)} %param.7) | copy-start | bytes 98308
  7.2 389.5 %all-gather.7.cloned.1.call-start = ((), (), s32[]{:S(2)}) async-start(), calls=%async_computation | async-start | bytes 15728640 | tf_op jit(solution)/shard_map/all_gather | solution.py:60
  14.3 23.8 %collective-permute-start = (bf16[96,32,128]{2,1,0:T(8,128)(2,1)}, bf16[96,32,128]{2,1,0:T(8,128)(2,1)S(1)}, u32[]{:S(2)}, u32[]{:S(2)}) collective-permute-start(bf16[96,32,128]{2,1,0:T(8,128)(2,1)} %get-tuple-element.51), channel_id=1, source_target_pairs={{0,4},{4,8},{8,12},{12,0},{1,5},{5,9},{9,13},{13,1},{2,6},{6,10},{... | collective-permute-start | bytes 2359304 | tf_op jit(solution)/shard_map/ppermute | solution.py:37
  18.9 52.2 %collective-permute-start.1 = (bf16[96,32,128]{2,1,0:T(8,128)(2,1)}, bf16[96,32,128]{2,1,0:T(8,128)(2,1)}, u32[]{:S(2)}, u32[]{:S(2)}) collective-permute-start(bf16[96,32,128]{2,1,0:T(8,128)(2,1)} %get-tuple-element.54), channel_id=1, source_target_pairs={{0,8},{4,12},{8,0},{12,4},{1,9},{5,13},{9,1},{13,5},{2,10},{6,14},... | collective-permute-start | bytes 2359304 | tf_op jit(solution)/shard_map/ppermute | solution.py:37
  23.0 48.1 %collective-permute-start.2 = (bf16[96,32,128]{2,1,0:T(8,128)(2,1)}, bf16[96,32,128]{2,1,0:T(8,128)(2,1)}, u32[]{:S(2)}, u32[]{:S(2)}) collective-permute-start(bf16[96,32,128]{2,1,0:T(8,128)(2,1)} %get-tuple-element.57), channel_id=1, source_target_pairs={{0,12},{4,0},{8,4},{12,8},{1,13},{5,1},{9,5},{13,9},{2,14},{6,2},{... | collective-permute-start | bytes 2359304 | tf_op jit(solution)/shard_map/ppermute | solution.py:37
  87.8 10.7 %copy-start.9 = (bf16[128,640]{1,0:T(8,128)(2,1)S(1)}, bf16[128,640]{1,0:T(8,128)(2,1)}, u32[]{:S(2)}) copy-start(bf16[128,640]{1,0:T(8,128)(2,1)} %param.6) | copy-start | bytes 491524
  107.7 358.2 %all-gather.9.cloned.1.call-start = ((), (), s32[]{:S(2)}) async-start(), calls=%async_computation.1 | async-start | bytes 15728640 | tf_op jit(solution)/shard_map/all_gather | solution.py:60
  107.7 75.4 %copy-start.8 = (bf16[96,32,128]{2,1,0:T(8,128)(2,1)S(1)}, bf16[96,32,128]{2,1,0:T(8,128)(2,1)}, u32[]{:S(2)}) copy-start(bf16[96,32,128]{2,1,0:T(8,128)(2,1)} %get-tuple-element.50) | copy-start | bytes 2359300
  107.8 37.1 %collective-permute-start.3 = (bf16[96,32,128]{2,1,0:T(8,128)(2,1)}, bf16[96,32,128]{2,1,0:T(8,128)(2,1)S(1)}, u32[]{:S(2)}, u32[]{:S(2)}) collective-permute-start(bf16[96,32,128]{2,1,0:T(8,128)(2,1)} %get-tuple-element.53), channel_id=1, source_target_pairs={{0,4},{4,8},{8,12},{12,0},{1,5},{5,9},{9,13},{13,1},{2,6},{6,10},{... | collective-permute-start | bytes 2359304 | tf_op jit(solution)/shard_map/ppermute | solution.py:37
  125.1 51.8 %collective-permute-start.4 = (bf16[96,32,128]{2,1,0:T(8,128)(2,1)}, bf16[96,32,128]{2,1,0:T(8,128)(2,1)S(1)}, u32[]{:S(2)}, u32[]{:S(2)}) collective-permute-start(bf16[96,32,128]{2,1,0:T(8,128)(2,1)} %get-tuple-element.56), channel_id=1, source_target_pairs={{0,8},{4,12},{8,0},{12,4},{1,9},{5,13},{9,1},{13,5},{2,10},{6,14},... | collective-permute-start | bytes 2359304 | tf_op jit(solution)/shard_map/ppermute | solution.py:37
  126.7 50.2 %collective-permute-start.5 = (bf16[96,32,128]{2,1,0:T(8,128)(2,1)}, bf16[96,32,128]{2,1,0:T(8,128)(2,1)S(1)}, u32[]{:S(2)}, u32[]{:S(2)}) collective-permute-start(bf16[96,32,128]{2,1,0:T(8,128)(2,1)} %get-tuple-element.59), channel_id=1, source_target_pairs={{0,12},{4,0},{8,4},{12,8},{1,13},{5,1},{9,5},{13,9},{2,14},{6,2},{... | collective-permute-start | bytes 2359304 | tf_op jit(solution)/shard_map/ppermute | solution.py:37
  221.5 286.8 %all-gather.11.cloned.1.call-start = ((), (), s32[]{:S(2)}) async-start(), calls=%async_computation.2 | async-start | bytes 15728640 | tf_op jit(solution)/shard_map/all_gather | solution.py:60
  221.5 37.9 %collective-permute-start.6 = (bf16[96,32,128]{2,1,0:T(8,128)(2,1)}, bf16[96,32,128]{2,1,0:T(8,128)(2,1)}, u32[]{:S(2)}, u32[]{:S(2)}) collective-permute-start(bf16[96,32,128]{2,1,0:T(8,128)(2,1)} %get-tuple-element.52), channel_id=1, source_target_pairs={{0,4},{4,8},{8,12},{12,0},{1,5},{5,9},{9,13},{13,1},{2,6},{6,10},{... | collective-permute-start | bytes 2359304 | tf_op jit(solution)/shard_map/ppermute | solution.py:37
  238.8 53.1 %collective-permute-start.7 = (bf16[96,32,128]{2,1,0:T(8,128)(2,1)}, bf16[96,32,128]{2,1,0:T(8,128)(2,1)}, u32[]{:S(2)}, u32[]{:S(2)}) collective-permute-start(bf16[96,32,128]{2,1,0:T(8,128)(2,1)} %get-tuple-element.55), channel_id=1, source_target_pairs={{0,8},{4,12},{8,0},{12,4},{1,9},{5,13},{9,1},{13,5},{2,10},{6,14},... | collective-permute-start | bytes 2359304 | tf_op jit(solution)/shard_map/ppermute | solution.py:37
  241.2 50.7 %collective-permute-start.8 = (bf16[96,32,128]{2,1,0:T(8,128)(2,1)}, bf16[96,32,128]{2,1,0:T(8,128)(2,1)}, u32[]{:S(2)}, u32[]{:S(2)}) collective-permute-start(bf16[96,32,128]{2,1,0:T(8,128)(2,1)} %get-tuple-element.58), channel_id=1, source_target_pairs={{0,12},{4,0},{8,4},{12,8},{1,13},{5,1},{9,5},{13,9},{2,14},{6,2},{... | collective-permute-start | bytes 2359304 | tf_op jit(solution)/shard_map/ppermute | solution.py:37
  241.3 54.2 %copy-start.7 = (bf16[96,32,128]{2,1,0:T(8,128)(2,1)S(1)}, bf16[96,32,128]{2,1,0:T(8,128)(2,1)}, u32[]{:S(2)}) copy-start(bf16[96,32,128]{2,1,0:T(8,128)(2,1)} %get-tuple-element.49) | copy-start | bytes 2359300
  332.4 26.8 %slice-start = ((s8[9437184]{0:T(1024)(128)(4,1)}), s8[4194304]{0:T(1024)(128)(4,1)S(1)}, s32[]{:S(2)}) async-start(s8[9437184]{0:T(1024)(128)(4,1)} %bitcast.396), calls=%async_computation.3 | async-start | bytes 8388608
  332.4 26.8 %slice-start.1 = ((s8[9437184]{0:T(1024)(128)(4,1)}), s8[1048576]{0:T(1024)(128)(4,1)S(1)}, s32[]{:S(2)}) async-start(s8[9437184]{0:T(1024)(128)(4,1)} %bitcast.396), calls=%async_computation.4 | async-start | bytes 2097152
  339.9 18.6 %copy-start.27 = (f32[96]{0:T(128)S(1)}, f32[96]{0:T(128)}, u32[]{:S(2)}) copy-start(f32[96]{0:T(128)} %get-tuple-element.132) | copy-start | bytes 1156
  339.9 19.3 %slice-start.2 = ((s8[9437184]{0:T(1024)(128)(4,1)}), s8[4194304]{0:T(1024)(128)(4,1)S(1)}, s32[]{:S(2)}) async-start(s8[9437184]{0:T(1024)(128)(4,1)} %bitcast.396), calls=%async_computation.5 | async-start | bytes 8388608
  443.3 146.5 %collective-permute-start.9 = (bf16[32,96,128]{2,1,0:T(8,128)(2,1)}, bf16[32,96,128]{2,1,0:T(8,128)(2,1)}, u32[]{:S(2)}, u32[]{:S(2)}) collective-permute-start(bf16[32,96,128]{2,1,0:T(8,128)(2,1)} %bitcast.407), channel_id=1, source_target_pairs={{0,4},{4,8},{8,12},{12,0},{1,5},{5,9},{9,13},{13,1},{2,6},{6,10},{... | collective-permute-start | bytes 2359304 | tf_op jit(solution)/shard_map/ppermute | solution.py:37
  461.5 134.5 %collective-permute-start.10 = (bf16[32,96,128]{2,1,0:T(8,128)(2,1)}, bf16[32,96,128]{2,1,0:T(8,128)(2,1)}, u32[]{:S(2)}, u32[]{:S(2)}) collective-permute-start(bf16[32,96,128]{2,1,0:T(8,128)(2,1)} %bitcast.22), channel_id=1, source_target_pairs={{0,8},{4,12},{8,0},{12,4},{1,9},{5,13},{9,1},{13,5},{2,10},{6,14},... | collective-permute-start | bytes 2359304 | tf_op jit(solution)/shard_map/ppermute | solution.py:37
  464.9 135.1 %collective-permute-start.11 = (bf16[32,96,128]{2,1,0:T(8,128)(2,1)}, bf16[32,96,128]{2,1,0:T(8,128)(2,1)}, u32[]{:S(2)}, u32[]{:S(2)}) collective-permute-start(bf16[32,96,128]{2,1,0:T(8,128)(2,1)} %bitcast.26), channel_id=1, source_target_pairs={{0,12},{4,0},{8,4},{12,8},{1,13},{5,1},{9,5},{13,9},{2,14},{6,2},{... | collective-permute-start | bytes 2359304 | tf_op jit(solution)/shard_map/ppermute | solution.py:37
  555.7 54.3 %collective-permute-start.12 = (bf16[32,96,128]{2,1,0:T(8,128)(2,1)}, bf16[32,96,128]{2,1,0:T(8,128)(2,1)}, u32[]{:S(2)}, u32[]{:S(2)}) collective-permute-start(bf16[32,96,128]{2,1,0:T(8,128)(2,1)} %bitcast.408), channel_id=1, source_target_pairs={{0,4},{4,8},{8,12},{12,0},{1,5},{5,9},{9,13},{13,1},{2,6},{6,10},{... | collective-permute-start | bytes 2359304 | tf_op jit(solution)/shard_map/ppermute | solution.py:37
  559.3 56.3 %collective-permute-start.13 = (bf16[32,96,128]{2,1,0:T(8,128)(2,1)}, bf16[32,96,128]{2,1,0:T(8,128)(2,1)}, u32[]{:S(2)}, u32[]{:S(2)}) collective-permute-start(bf16[32,96,128]{2,1,0:T(8,128)(2,1)} %bitcast.406), channel_id=1, source_target_pairs={{0,8},{4,12},{8,0},{12,4},{1,9},{5,13},{9,1},{13,5},{2,10},{6,14},... | collective-permute-start | bytes 2359304 | tf_op jit(solution)/shard_map/ppermute | solution.py:37
  589.8 53.7 %collective-permute-start.14 = (bf16[32,96,128]{2,1,0:T(8,128)(2,1)}, bf16[32,96,128]{2,1,0:T(8,128)(2,1)S(1)}, u32[]{:S(2)}, u32[]{:S(2)}) collective-permute-start(bf16[32,96,128]{2,1,0:T(8,128)(2,1)} %bitcast.409), channel_id=1, source_target_pairs={{0,12},{4,0},{8,4},{12,8},{1,13},{5,1},{9,5},{13,9},{2,14},{6,2},{... | collective-permute-start | bytes 2359304 | tf_op jit(solution)/shard_map/ppermute | solution.py:37
  596.0 55.0 %collective-permute-start.15 = (bf16[32,96,128]{2,1,0:T(8,128)(2,1)S(1)}, bf16[32,96,128]{2,1,0:T(8,128)(2,1)S(1)}, u32[]{:S(2)}, u32[]{:S(2)}) collective-permute-start(bf16[32,96,128]{2,1,0:T(8,128)(2,1)S(1)} %bitcast.405), channel_id=1, source_target_pairs={{0,4},{4,8},{8,12},{12,0},{1,5},{5,9},{9,13},{13,1},{2,6},{6,10},{... | collective-permute-start | bytes 2359304 | tf_op jit(solution)/shard_map/ppermute | solution.py:37
  600.0 77.6 %collective-permute-start.16 = (bf16[32,96,128]{2,1,0:T(8,128)(2,1)S(1)}, bf16[32,96,128]{2,1,0:T(8,128)(2,1)S(1)}, u32[]{:S(2)}, u32[]{:S(2)}) collective-permute-start(bf16[32,96,128]{2,1,0:T(8,128)(2,1)S(1)} %bitcast.404), channel_id=1, source_target_pairs={{0,8},{4,12},{8,0},{12,4},{1,9},{5,13},{9,1},{13,5},{2,10},{6,14},... | collective-permute-start | bytes 2359304 | tf_op jit(solution)/shard_map/ppermute | solution.py:37
  610.0 70.3 %collective-permute-start.17 = (bf16[32,96,128]{2,1,0:T(8,128)(2,1)S(1)}, bf16[32,96,128]{2,1,0:T(8,128)(2,1)S(1)}, u32[]{:S(2)}, u32[]{:S(2)}) collective-permute-start(bf16[32,96,128]{2,1,0:T(8,128)(2,1)S(1)} %bitcast.403), channel_id=1, source_target_pairs={{0,12},{4,0},{8,4},{12,8},{1,13},{5,1},{9,5},{13,9},{2,14},{6,2},{... | collective-permute-start | bytes 2359304 | tf_op jit(solution)/shard_map/ppermute | solution.py:37
  615.6 27.9 %copy-start.15 = (f32[32,96,128]{2,1,0:T(8,128)S(1)}, f32[32,96,128]{2,1,0:T(8,128)}, u32[]{:S(2)}) copy-start(f32[32,96,128]{2,1,0:T(8,128)} %fusion.150) | copy-start | bytes 4718596
  651.0 26.6 %copy-start.13 = (f32[32,96,128]{2,1,0:T(8,128)S(1)}, f32[32,96,128]{2,1,0:T(8,128)}, u32[]{:S(2)}) copy-start(f32[32,96,128]{2,1,0:T(8,128)} %fusion.155) | copy-start | bytes 4718596
  651.0 26.6 %copy-start.22 = (f32[32,96]{1,0:T(8,128)S(1)}, f32[32,96]{1,0:T(8,128)}, u32[]{:S(2)}) copy-start(f32[32,96]{1,0:T(8,128)} %get-tuple-element.72) | copy-start | bytes 36868
  (23 other events, 119.5 us)
Sparse Core Ops, SparseCore 0:
  107.8 138.3 all-gather.6
  248.1 122.3 all-gather.8
  372.3 122.3 all-gather.10

commit v2 on v0

--- a/solution.py
+++ b/solution.py
@@ -1,17 +1,459 @@
+import functools
+
 import jax
 import jax.numpy as jnp
 from jax import lax
+from jax.experimental import pallas as pl
+from jax.experimental.pallas import tpu as pltpu
 from jax.sharding import PartitionSpec as P
+
+WIDTH = 16
+UNROLL = 2
+LANES = 128
+EPS = 1e-05
 
 
 def layer_norm(values):
     mean_value = jnp.mean(values, axis=-1, keepdims=True)
     centered = values - mean_value
     variance = jnp.mean(centered * centered, axis=-1, keepdims=True)
-    return centered * lax.rsqrt(variance + 1e-05)
-
-
-def per_device(pair_repr, seq_lengths, weight_in, weight_out):
+    return centered * lax.rsqrt(variance + EPS)
+
+
+def contract_last(a, b):
+    return lax.dot_general(a, b, (((1,), (1,)), ((), ())), preferred_element_type=jnp.float32)
+
+
+def meet(axes):
+    barrier = pltpu.get_barrier_semaphore()
+    for axis, size in axes:
+        me = lax.axis_index(axis)
+        for s in range(1, size):
+            pl.semaphore_signal(
+                barrier, inc=1, device_id={axis: lax.rem(me + s, size)},
+                device_id_type=pl.DeviceIdType.MESH,
+            )
+    pl.semaphore_wait(barrier, sum(size - 1 for _, size in axes))
+
+
+def remote(src, dst, send, recv, axis, target):
+    return pltpu.make_async_remote_copy(
+        src_ref=src, dst_ref=dst, send_sem=send, recv_sem=recv,
+        device_id={axis: target}, device_id_type=pl.DeviceIdType.MESH,
+    )
+
+
+def enter_kernel(
+    ring, pair_ref, weight_ref, mask_ref, sides_ref, got_ref,
+    block, stage, ready, load_sem, z_send, z_recv, y_send, y_recv, own_sem,
+):
+    me, col = lax.axis_index("gx"), lax.axis_index("gy")
+    cols, rows = pair_ref.shape[1], pair_ref.shape[2]
+    hidden = weight_ref.shape[0] // 4
+    quarter = hidden // ring
+    steps = cols // WIDTH
+    deep = ring * rows
+    meet((("gx", ring), ("gy", ring)))
+
+    def inbound(t, s):
+        target = jnp.bitwise_xor(me, s)
+        part = pl.ds(pl.multiple_of(t * WIDTH, WIDTH), WIDTH)
+        return remote(
+            pair_ref.at[target, part], got_ref.at[s - 1, part],
+            z_send.at[t, s - 1], z_recv.at[t, s - 1], "gx", target,
+        )
+
+    def outbound(t, s):
+        target = jnp.bitwise_xor(col, s)
+        return remote(
+            ready.at[lax.rem(t, 2), target], sides_ref.at[t, col],
+            y_send.at[t, s - 1], y_recv.at[t, s - 1], "gy", target,
+        )
+
+    def own(t):
+        return pltpu.make_async_copy(
+            ready.at[lax.rem(t, 2), col], sides_ref.at[t, col], own_sem.at[t]
+        )
+
+    for t in range(steps):
+        for s in range(1, ring):
+            inbound(t, s).start()
+
+    def drain(t):
+        for s in range(1, ring):
+            outbound(t, s).wait_send()
+        own(t).wait()
+
+    def step(t, carry):
+        for s in range(1, ring):
+            inbound(t, s).wait_recv()
+        part = pl.ds(pl.multiple_of(t * WIDTH, WIDTH), WIDTH)
+        loads = []
+        for s in range(ring):
+            src = pair_ref.at[me, part] if s == 0 else got_ref.at[s - 1, part]
+            loads.append(
+                pltpu.make_async_copy(src, block.at[:, pl.ds(s * rows, rows)], load_sem.at[s])
+            )
+            loads[-1].start()
+        for load in loads:
+            load.wait()
+
+        def column(i, carry):
+            normed = layer_norm(block[i].astype(jnp.float32)).astype(jnp.bfloat16)
+            proj = contract_last(weight_ref[...], normed)
+            live = mask_ref[pl.ds(t * WIDTH + i, 1), :]
+            for side in range(2):
+                first = 2 * side * hidden
+                value = proj[first : first + hidden]
+                gate = proj[first + hidden : first + 2 * hidden]
+                out = live * jax.nn.sigmoid(gate) * value
+                for l in range(deep // LANES):
+                    stage[l, pl.ds(side * hidden * WIDTH + i, hidden, stride=WIDTH), :] = out[
+                        :, l * LANES : (l + 1) * LANES
+                    ]
+            return carry
+
+        lax.fori_loop(0, WIDTH, column, 0, unroll=UNROLL)
+
+        @pl.when(t >= 2)
+        def _():
+            drain(t - 2)
+
+        slot = lax.rem(t, 2)
+        for side in range(2):
+            for q in range(ring):
+                first = (side * hidden + q * quarter) * WIDTH
+                for l in range(deep // LANES):
+                    ready[slot, q, side, :, :, l * LANES : (l + 1) * LANES] = (
+                        stage[l, first : first + quarter * WIDTH, :]
+                        .reshape(quarter, WIDTH, LANES)
+                        .astype(jnp.bfloat16)
+                    )
+        for s in range(1, ring):
+            outbound(t, s).start()
+        own(t).start()
+        return carry
+
+    lax.fori_loop(0, steps, step, 0)
+    for t in range(max(steps - 2, 0), steps):
+        drain(t)
+    for t in range(steps):
+        for s in range(1, ring):
+            inbound(t, s).wait_send()
+            outbound(t, s).wait_recv()
+
+
+def leave_kernel(
+    ring, pairs, sides_ref, pair_ref, gate_ref, out_ref, live_ref, col_ref,
+    updated_ref, total_ref, tri_ref, home_ref,
+    left, right, product, part_ref, stage, normed_ref, home, pair, result, sums, boxes,
+    load_sem, y_send, y_recv, y_own, z_send, z_recv, z_own, keep_sem, sum_send, sum_recv, side_sem,
+):
+    me, col = lax.axis_index("gx"), lax.axis_index("gy")
+    cols, rows, channels = pair_ref.shape[1:]
+    quarter = sides_ref.shape[3]
+    hidden = ring * quarter
+    steps = cols // WIDTH
+    wide = ring * rows
+    axes = (("gx", ring), ("gy", ring), ("gz", pairs))
+    meet(axes)
+
+    def part(t):
+        return pl.ds(pl.multiple_of(t * WIDTH, WIDTH), WIDTH)
+
+    def across(t, s):
+        target = jnp.bitwise_xor(col, s)
+        return remote(
+            product.at[lax.rem(t, 2), target], tri_ref.at[t, col],
+            y_send.at[t, s - 1], y_recv.at[t, s - 1], "gy", target,
+        )
+
+    def across_own(t):
+        return pltpu.make_async_copy(
+            product.at[lax.rem(t, 2), col], tri_ref.at[t, col], y_own.at[t]
+        )
+
+    def homeward(t, s):
+        target = jnp.bitwise_xor(me, s)
+        return remote(
+            normed_ref.at[lax.rem(t, 2), target], home_ref.at[me, part(t)],
+            z_send.at[t, s - 1], z_recv.at[t, s - 1], "gx", target,
+        )
+
+    def homeward_own(t):
+        return pltpu.make_async_copy(
+            normed_ref.at[lax.rem(t, 2), me], home_ref.at[me, part(t)], z_own.at[t]
+        )
+
+    def keep(t):
+        return pltpu.make_async_copy(result, updated_ref.at[:, part(t)], keep_sem)
+
+    loads = [
+        pltpu.make_async_copy(
+            sides_ref.at[t, g, side], keeper.at[:, pl.ds(g * cols + t * WIDTH, WIDTH)],
+            side_sem.at[t, g, side],
+        )
+        for t in range(steps)
+        for g in range(ring)
+        for side, keeper in enumerate((left, right))
+    ]
+    for load in loads:
+        load.start()
+    total_ref[...] = jnp.zeros_like(total_ref)
+    for load in loads:
+        load.wait()
+
+    def multiply(t):
+        @pl.when(t >= 2)
+        def _():
+            for s in range(1, ring):
+                across(t - 2, s).wait_send()
+
+        slot = lax.rem(t, 2)
+
+        def channel(c, carry):
+            rights = jnp.concatenate(
+                [
+                    right[c, pl.ds(pl.multiple_of(g * cols + t * WIDTH, WIDTH), WIDTH), :]
+                    for g in range(ring)
+                ],
+                axis=0,
+            )
+            found = contract_last(rights, left[c]).astype(jnp.bfloat16)
+            for g in range(ring):
+                product[slot, g, c] = found[g * WIDTH : (g + 1) * WIDTH]
+            return carry
+
+        lax.fori_loop(0, quarter, channel, 0, unroll=UNROLL)
+        for s in range(1, ring):
+            across(t, s).start()
+        across_own(t).start()
+
+    def normalise(t):
+        for s in range(1, ring):
+            across(t, s).wait_recv()
+        across_own(t).wait()
+        load = pltpu.make_async_copy(tri_ref.at[t], part_ref, load_sem.at[0])
+        load.start()
+
+        @pl.when(t >= 2)
+        def _():
+            for s in range(1, ring):
+                homeward(t - 2, s).wait_send()
+            homeward_own(t - 2).wait()
+
+        load.wait()
+        for q in range(ring):
+            for l in range(wide // LANES):
+                stage[l, q * quarter * WIDTH : (q + 1) * quarter * WIDTH, :] = (
+                    part_ref[q, :, :, l * LANES : (l + 1) * LANES]
+                    .astype(jnp.float32)
+                    .reshape(quarter * WIDTH, LANES)
+                )
+        slot = lax.rem(t, 2)
+
+        def column(j, carry):
+            for l in range(wide // LANES):
+                values = stage[l, pl.ds(j, hidden, stride=WIDTH), :]
+                centered = values - jnp.mean(values, axis=0, keepdims=True)
+                variance = jnp.mean(centered * centered, axis=0, keepdims=True)
+                scaled = centered * lax.rsqrt(variance + EPS)
+                turned = scaled.T.astype(jnp.bfloat16)
+                for g in range(ring):
+                    low, high = max(g * rows, l * LANES), min((g + 1) * rows, (l + 1) * LANES)
+                    if low < high:
+                        normed_ref[slot, g, j, low - g * rows : high - g * rows, :] = turned[
+                            low - l * LANES : high - l * LANES
+                        ]
+            return carry
+
+        lax.fori_loop(0, WIDTH, column, 0, unroll=UNROLL)
+        for s in range(1, ring):
+            homeward(t, s).start()
+        homeward_own(t).start()
+
+    def finish(t):
+        own_load = pltpu.make_async_copy(pair_ref.at[:, part(t)], pair, load_sem.at[1])
+        own_load.start()
+        for s in range(1, ring):
+            homeward(t, s).wait_recv()
+
+        @pl.when(t >= steps - 2)
+        def _():
+            homeward_own(t).wait()
+
+        home_load = pltpu.make_async_copy(home_ref.at[:, part(t)], home, load_sem.at[0])
+        home_load.start()
+
+        @pl.when(t >= 1)
+        def _():
+            keep(t - 1).wait()
+
+        own_load.wait()
+        home_load.wait()
+
+        def column(j, carry):
+            for b in range(ring):
+                own = pair[b, j].astype(jnp.float32)
+                normed = layer_norm(own).astype(jnp.bfloat16)
+                gate = jax.nn.sigmoid(
+                    jnp.dot(normed, gate_ref[...], preferred_element_type=jnp.float32)
+                )
+                back = jnp.dot(home[b, j], out_ref[...], preferred_element_type=jnp.float32)
+                live = live_ref[b] * col_ref[b, t * WIDTH + j]
+                one = (own + live * gate * back).astype(jnp.bfloat16)
+                result[b, j] = one
+                size = jnp.abs(one.astype(jnp.float32)).reshape(rows // 8, 8, channels)
+                total_ref[...] += jnp.sum(size, axis=0)
+            return carry
+
+        lax.fori_loop(0, WIDTH, column, 0, unroll=UNROLL)
+        keep(t).start()
+
+    lag = 3
+
+    def step(t, carry):
+        @pl.when(t < steps)
+        def _():
+            multiply(t)
+
+        @pl.when(jnp.logical_and(t >= 1, t < steps + 1))
+        def _():
+            normalise(t - 1)
+
+        @pl.when(t >= lag)
+        def _():
+            finish(t - lag)
+
+        return carry
+
+    lax.fori_loop(0, steps + lag, step, 0)
+    sending = []
+    for phase, (axis, size) in enumerate(axes):
+        here = lax.axis_index(axis)
+        sums[phase] = total_ref[...]
+        boxes[phase, here] = total_ref[...]
+        copies = [
+            remote(
+                sums.at[phase], boxes.at[phase, here], sum_send.at[phase, s - 1],
+                sum_recv.at[phase, s - 1], axis, lax.rem(here + s, size),
+            )
+            for s in range(1, size)
+        ]
+        for copy in copies:
+            copy.start()
+        for copy in copies:
+            copy.wait_recv()
+        total_ref[...] = jnp.sum(boxes[phase, :size], axis=0)
+        sending += copies
+    for copy in sending:
+        copy.wait_send()
+    keep(steps - 1).wait()
+    for t in range(max(steps - 2, 0), steps):
+        for s in range(1, ring):
+            across(t, s).wait_send()
+            homeward(t, s).wait_send()
+
+
+def rehomed(pair_repr, seq_lengths, weight_in, weight_out):
+    ring, rows, cols, channels = pair_repr.shape
+    hidden = weight_out.shape[0]
+    quarter = hidden // ring
+    steps = cols // WIDTH
+    deep = ring * rows
+    pairs = lax.axis_size("gz")
+    most = max(ring, pairs)
+    me = lax.axis_index("gx")
+    row_first = me * rows
+    col_first = lax.axis_index("gy") * cols
+    lengths = lax.dynamic_slice_in_dim(seq_lengths, lax.axis_index("gz") * ring, ring)
+    length = lax.dynamic_index_in_dim(lengths, me, 0, keepdims=False)
+    row_local = jnp.arange(rows, dtype=jnp.int32)
+    col_at = col_first + jnp.arange(cols, dtype=jnp.int32)
+    k_at = jnp.concatenate([jnp.bitwise_xor(me, s) * rows + row_local for s in range(ring)])
+    mask = ((col_at < length)[:, None] & (k_at < length)[None, :]).astype(jnp.float32)
+    row_live = ((row_first + row_local)[None, :] < lengths[:, None]).astype(jnp.float32)
+    row_live = jnp.broadcast_to(row_live[:, :, None], (ring, rows, channels))
+    col_live = (col_at[None, :] < lengths[:, None]).astype(jnp.float32)
+    pair_t = pair_repr.transpose(0, 2, 1, 3)
+    weight_t = weight_in[:, : 4 * hidden].T
+    any_space = pl.BlockSpec(memory_space=pl.ANY)
+    vmem = pl.BlockSpec(memory_space=pltpu.VMEM)
+    smem = pl.BlockSpec(memory_space=pltpu.SMEM)
+    dma = pltpu.SemaphoreType.DMA
+    f32, bf16 = jnp.float32, jnp.bfloat16
+
+    sides, _ = pl.pallas_call(
+        functools.partial(enter_kernel, ring),
+        out_shape=(
+            jax.ShapeDtypeStruct((steps, ring, 2, quarter, WIDTH, deep), bf16),
+            jax.ShapeDtypeStruct((ring - 1, cols, rows, channels), bf16),
+        ),
+        in_specs=[any_space, vmem, vmem],
+        out_specs=(any_space, any_space),
+        scratch_shapes=[
+            pltpu.VMEM((WIDTH, deep, channels), bf16),
+            pltpu.VMEM((deep // LANES, 2 * hidden * WIDTH, LANES), f32),
+            pltpu.VMEM((2, ring, 2, quarter, WIDTH, deep), bf16),
+            dma((ring,)),
+            dma((steps, ring - 1)),
+            dma((steps, ring - 1)),
+            dma((steps, ring - 1)),
+            dma((steps, ring - 1)),
+            dma((steps,)),
+        ],
+        compiler_params=pltpu.CompilerParams(
+            collective_id=0, has_side_effects=True, vmem_limit_bytes=60 * 1024 * 1024
+        ),
+        name="enter",
+    )(pair_t, weight_t, mask)
+
+    updated_t, total, _, _ = pl.pallas_call(
+        functools.partial(leave_kernel, ring, pairs),
+        out_shape=(
+            jax.ShapeDtypeStruct(pair_t.shape, bf16),
+            jax.ShapeDtypeStruct((8, channels), f32),
+            jax.ShapeDtypeStruct((steps, ring, quarter, WIDTH, ring * rows), bf16),
+            jax.ShapeDtypeStruct((ring, cols, rows, channels), bf16),
+        ),
+        in_specs=[any_space, any_space, vmem, vmem, vmem, smem],
+        out_specs=(any_space, vmem, any_space, any_space),
+        scratch_shapes=[
+            pltpu.VMEM((quarter, ring * cols, deep), bf16),
+            pltpu.VMEM((quarter, ring * cols, deep), bf16),
+            pltpu.VMEM((2, ring, quarter, WIDTH, ring * rows), bf16),
+            pltpu.VMEM((ring, quarter, WIDTH, ring * rows), bf16),
+            pltpu.VMEM((ring * rows // LANES, hidden * WIDTH, LANES), f32),
+            pltpu.VMEM((2, ring, WIDTH, rows, channels), bf16),
+            pltpu.VMEM((ring, WIDTH, rows, channels), bf16),
+            pltpu.VMEM((ring, WIDTH, rows, channels), bf16),
+            pltpu.VMEM((ring, WIDTH, rows, channels), bf16),
+            pltpu.VMEM((3, 8, channels), f32),
+            pltpu.VMEM((3, most, 8, channels), f32),
+            dma((2,)),
+            dma((steps, ring - 1)),
+            dma((steps, ring - 1)),
+            dma((steps,)),
+            dma((steps, ring - 1)),
+            dma((steps, ring - 1)),
+            dma((steps,)),
+            dma(()),
+            dma((3, most - 1)),
+            dma((3, most - 1)),
+            dma((steps, ring, 2)),
+        ],
+        compiler_params=pltpu.CompilerParams(
+            collective_id=1, has_side_effects=True, vmem_limit_bytes=60 * 1024 * 1024
+        ),
+        name="leave",
+    )(sides, pair_t, weight_in[:, 4 * hidden :], weight_out, row_live, col_live)
+
+    updated = updated_t.transpose(0, 2, 1, 3)
+    entry_count = ring * pairs * rows * ring * cols * lax.axis_size("gy") * channels
+    return (updated, jnp.sum(total) / float(entry_count))
+
+
+def gathered_columns(pair_repr, seq_lengths, weight_in, weight_out):
     batch_dev, row_count, col_count, channels = pair_repr.shape
     hidden = weight_out.shape[0]
     row_first = lax.axis_index("gx") * row_count
@@ -72,6 +514,15 @@
     return (updated, magnitude)
 
 
+def per_device(pair_repr, seq_lengths, weight_in, weight_out):
+    ring, rows, cols, channels = pair_repr.shape
+    square = lax.axis_size("gx") == ring and lax.axis_size("gy") == ring and ring & (ring - 1) == 0
+    tiled = rows % WIDTH == 0 and cols % WIDTH == 0 and ring * rows % LANES == 0
+    if square and tiled and channels == LANES and weight_out.shape[0] == LANES:
+        return rehomed(pair_repr, seq_lengths, weight_in, weight_out)
+    return gathered_columns(pair_repr, seq_lengths, weight_in, weight_out)
+
+
 def solution(mesh):
     return jax.shard_map(
         per_device,

time: 1190 us -> 582 us (0.49)
  waiting for transfers between devices: 772 us -> 0 us
  Pallas kernels: 0 us -> 546 us
  matrix products: 139 us -> 0 us
  local copies, waits for them, and re-layouts: 126 us -> 28 us
  other arithmetic: 82.6 us -> 4.08 us
  blocking collectives: 41.2 us -> 0 us
  between operations: 19.6 us -> 2.47 us
    reduce_scatter x4 -> x0, waiting for transfers between devices: 563 us -> none  [per_device(): lax.psum_scatter(partial, 'gx', scatter_dimension=0, tiled=True)]
    pallas_call x0 -> x2, Pallas kernels: none -> 546 us  [the longest x1 281 us: rehomed(): pl.pallas_call(functools.partial(enter_kernel, ring), out_shape=(jax.Shap...]
    all_gather x4 -> x0, waiting for transfers between devices: 209 us -> none  [per_device(): gathered.append(lax.all_gather(left, 'gy', axis=1, tiled=True))]
    dot_general x20 -> x0, matrix products: 139 us -> none  [the longest x8 51.6 us: gated(): jnp.einsum('ijc,cd->ijd', normed, part, preferred_element_type=jnp.float32)]
    convert_element_type x8 -> x0, local copies, waits for them, and re-layouts: 72.3 us -> none  [the longest x4 55.6 us: per_device(): partial = jnp.einsum('kic,kjc->ijc', gathered[b], right, preferred_elemen...]
    all_gather x4 -> x0, local copies, waits for them, and re-layouts: 52.1 us -> none  [per_device(): gathered.append(lax.all_gather(left, 'gy', axis=1, tiled=True))]
    reduce_sum x10 -> x1, other arithmetic: 46.9 us -> 1.28 us  [rehomed(): return (updated, jnp.sum(total) / float(entry_count))]
    psum x1 -> x0, blocking collectives: 41.2 us -> none  [per_device(): mag_total = lax.psum(total, ('gz', 'gx', 'gy'))]
  transfers between devices with their start and end apart: 8 -> 0, of which waited for: 8 -> 0; matrix products, arithmetic and copies ran while one was open for 23% -> 0% of each run, Pallas kernels for 0% -> 0%
where the time goes in v2:
time: 582 us; the launch traced here: 581 us
  Pallas kernels  546 us (94%)
  local copies, waits for them, and re-layouts  28 us (5%)
    pallas_call x1, Pallas kernels, rehomed(): pl.pallas_call(functools.partial(enter_kernel, ring), out_shape=(jax.Shap...  281 us
    pallas_call x1, Pallas kernels, rehomed(): pl.pallas_call(functools.partial(leave_kernel, ring, pairs), out_shape=(j...  266 us
    unnamed x3, local copies, waits for them, and re-layouts  22.9 us

profile of v2, /device:TPU:0, one launch (start us, length us, event | category | flops | bytes accessed | tf_op | source)
XLA Modules:
  0.0 580.9 jit_solution(15958114869165357907)
XLA Ops:
  0.7 1.2 dynamic_slice.10
  1.9 0.7 dynamic_slice.11
  2.6 0.7 add_compare_fusion
  3.4 0.7 broadcast_compare_fusion
  4.0 0.7 compare_convert_fusion
  4.7 1.4 slice.7.gate_ref
  6.1 0.9 slice.6
  7.0 0.7 copy.9
  7.7 0.7 and_convert_fusion.mask_ref
  8.5 0.8 broadcast_in_dim.2.live_ref
  9.3 11.1 %copy.11 = bf16[4,96,96,128]{3,1,2,0:T(8,128)(2,1)} copy(bf16[4,96,96,128]{3,2,1,0:T(8,128)(2,1)} %param.4) | data formatting | bytes 18874368 | tf_op args[0]
  20.3 280.8 %enter.1 = (bf16[6,4,2,32,16,384]{5,4,3,2,1,0:T(8,128)(2,1)}, bf16[3,96,96,128]{3,2,1,0:T(8,128)(2,1)}) custom-call(bf16[4,96,96,128]{3,2,1,0:T(8,128)(2,1)} %bitcast.6, bf16[512,128]{1,0:T(8,128)(2,1)} %bitcast.9, f32[96,384]{1,0:T(8,128)} %and_convert_fusion.mask_ref), custom_call_target="tpu_custom_call" | custom-call | tf_op jit(solution)/shard_map/enter/pallas_call | solution.py:386
  301.2 265.5 %leave.1 = (bf16[4,96,96,128]{3,2,1,0:T(8,128)(2,1)}, f32[8,128]{1,0:T(8,128)}, bf16[6,4,32,16,384]{4,3,2,1,0:T(8,128)(2,1)}, bf16[4,96,96,128]{3,2,1,0:T(8,128)(2,1)}) custom-call(bf16[6,4,2,32,16,384]{5,4,3,2,1,0:T(8,128)(2,1)} %get-tuple-element.5.sides_ref, bf16[4,96,96,128]{3,2,1,0:T(8,128)(2,1)} %bitcast.7, bf16[128,128]{1,0:T(8,128)(2,1)} %slice.7.gate_ref, ...), custom_call_target="tpu_custom_call" | custom-call | tf_op jit(solution)/shard_map/leave/pallas_call | solution.py:411
  566.7 1.3 reduce_sum.9
  568.6 11.1 %copy.8 = bf16[4,96,96,128]{3,2,1,0:T(8,128)(2,1)} copy(bf16[4,96,96,128]{3,1,2,0:T(8,128)(2,1)} %bitcast.8) | data formatting | bytes 18874368
  (3 shorter events, 0.0 us)

commit v3 on v2

--- a/solution.py
+++ b/solution.py
@@ -9,6 +9,7 @@
 
 WIDTH = 16
 UNROLL = 2
+WINDOW = 1
 LANES = 128
 EPS = 1e-05
 
@@ -43,63 +44,78 @@
     )
 
 
-def enter_kernel(
-    ring, pair_ref, weight_ref, mask_ref, sides_ref, got_ref,
-    block, stage, ready, load_sem, z_send, z_recv, y_send, y_recv, own_sem,
+def whole_kernel(
+    ring, pairs, pair_ref, weight_ref, gate_ref, out_ref, mask_ref, live_ref, col_ref,
+    updated_ref, total_ref, got_ref, tri_ref, home_ref,
+    block, turn, stage, ready, left, right, product, part_ref, normed_ref, home, pair, result,
+    sums, boxes,
+    load_sem, in_send, in_recv, side_send, side_recv, side_own, y_send, y_recv, y_own,
+    z_send, z_recv, z_own, keep_sem, sum_send, sum_recv,
 ):
     me, col = lax.axis_index("gx"), lax.axis_index("gy")
-    cols, rows = pair_ref.shape[1], pair_ref.shape[2]
+    rows, cols, channels = pair_ref.shape[1:]
     hidden = weight_ref.shape[0] // 4
     quarter = hidden // ring
     steps = cols // WIDTH
     deep = ring * rows
-    meet((("gx", ring), ("gy", ring)))
+    wide = ring * rows
+    tall = rows * WIDTH
+    axes = (("gx", ring), ("gy", ring), ("gz", pairs))
+    meet(axes)
+
+    def part(t):
+        return pl.ds(pl.multiple_of(t * WIDTH, WIDTH), WIDTH)
 
     def inbound(t, s):
         target = jnp.bitwise_xor(me, s)
-        part = pl.ds(pl.multiple_of(t * WIDTH, WIDTH), WIDTH)
         return remote(
-            pair_ref.at[target, part], got_ref.at[s - 1, part],
-            z_send.at[t, s - 1], z_recv.at[t, s - 1], "gx", target,
-        )
-
-    def outbound(t, s):
+            pair_ref.at[target, :, part(t)], got_ref.at[t, s - 1],
+            in_send.at[t, s - 1], in_recv.at[t, s - 1], "gx", target,
+        )
+
+    def place(t):
+        return pl.ds(pl.multiple_of(col * cols + t * WIDTH, WIDTH), WIDTH)
+
+    def outbound(t, s, side):
         target = jnp.bitwise_xor(col, s)
         return remote(
-            ready.at[lax.rem(t, 2), target], sides_ref.at[t, col],
-            y_send.at[t, s - 1], y_recv.at[t, s - 1], "gy", target,
-        )
-
-    def own(t):
-        return pltpu.make_async_copy(
-            ready.at[lax.rem(t, 2), col], sides_ref.at[t, col], own_sem.at[t]
-        )
-
-    for t in range(steps):
+            ready.at[lax.rem(t, 2), target, side], (left, right)[side].at[:, place(t)],
+            side_send.at[t, s - 1, side], side_recv.at[t, s - 1, side], "gy", target,
+        )
+
+    for t in range(min(WINDOW, steps)):
         for s in range(1, ring):
             inbound(t, s).start()
 
     def drain(t):
-        for s in range(1, ring):
-            outbound(t, s).wait_send()
-        own(t).wait()
-
-    def step(t, carry):
+        for side in range(2):
+            for s in range(1, ring):
+                outbound(t, s, side).wait_send()
+
+    def gather(t, carry):
         for s in range(1, ring):
             inbound(t, s).wait_recv()
-        part = pl.ds(pl.multiple_of(t * WIDTH, WIDTH), WIDTH)
+
+        @pl.when(t + WINDOW < steps)
+        def _():
+            for s in range(1, ring):
+                inbound(t + WINDOW, s).start()
+
         loads = []
         for s in range(ring):
-            src = pair_ref.at[me, part] if s == 0 else got_ref.at[s - 1, part]
+            src = pair_ref.at[me, :, part(t)] if s == 0 else got_ref.at[t, s - 1]
             loads.append(
-                pltpu.make_async_copy(src, block.at[:, pl.ds(s * rows, rows)], load_sem.at[s])
+                pltpu.make_async_copy(src, block.at[pl.ds(s * rows, rows)], load_sem.at[s])
             )
             loads[-1].start()
-        for load in loads:
-            load.wait()
+        for s in range(ring):
+            loads[s].wait()
+            turn[s * tall : (s + 1) * tall, :] = (
+                block[s * rows : (s + 1) * rows].astype(jnp.float32).reshape(tall, channels)
+            )
 
         def column(i, carry):
-            normed = layer_norm(block[i].astype(jnp.float32)).astype(jnp.bfloat16)
+            normed = layer_norm(turn[pl.ds(i, deep, stride=WIDTH), :]).astype(jnp.bfloat16)
             proj = contract_last(weight_ref[...], normed)
             live = mask_ref[pl.ds(t * WIDTH + i, 1), :]
             for side in range(2):
@@ -129,37 +145,12 @@
                         .reshape(quarter, WIDTH, LANES)
                         .astype(jnp.bfloat16)
                     )
-        for s in range(1, ring):
-            outbound(t, s).start()
-        own(t).start()
+            for s in range(1, ring):
+                outbound(t, s, side).start()
+            (left, right)[side][:, place(t)] = ready[slot, col, side]
         return carry
 
-    lax.fori_loop(0, steps, step, 0)
-    for t in range(max(steps - 2, 0), steps):
-        drain(t)
-    for t in range(steps):
-        for s in range(1, ring):
-            inbound(t, s).wait_send()
-            outbound(t, s).wait_recv()
-
-
-def leave_kernel(
-    ring, pairs, sides_ref, pair_ref, gate_ref, out_ref, live_ref, col_ref,
-    updated_ref, total_ref, tri_ref, home_ref,
-    left, right, product, part_ref, stage, normed_ref, home, pair, result, sums, boxes,
-    load_sem, y_send, y_recv, y_own, z_send, z_recv, z_own, keep_sem, sum_send, sum_recv, side_sem,
-):
-    me, col = lax.axis_index("gx"), lax.axis_index("gy")
-    cols, rows, channels = pair_ref.shape[1:]
-    quarter = sides_ref.shape[3]
-    hidden = ring * quarter
-    steps = cols // WIDTH
-    wide = ring * rows
-    axes = (("gx", ring), ("gy", ring), ("gz", pairs))
-    meet(axes)
-
-    def part(t):
-        return pl.ds(pl.multiple_of(t * WIDTH, WIDTH), WIDTH)
+    lax.fori_loop(0, steps, gather, 0)
 
     def across(t, s):
         target = jnp.bitwise_xor(col, s)
@@ -186,24 +177,17 @@
         )
 
     def keep(t):
-        return pltpu.make_async_copy(result, updated_ref.at[:, part(t)], keep_sem)
-
-    loads = [
-        pltpu.make_async_copy(
-            sides_ref.at[t, g, side], keeper.at[:, pl.ds(g * cols + t * WIDTH, WIDTH)],
-            side_sem.at[t, g, side],
-        )
-        for t in range(steps)
-        for g in range(ring)
-        for side, keeper in enumerate((left, right))
-    ]
-    for load in loads:
-        load.start()
+        return pltpu.make_async_copy(result, updated_ref.at[:, :, part(t)], keep_sem)
+
     total_ref[...] = jnp.zeros_like(total_ref)
-    for load in loads:
-        load.wait()
+    for t in range(steps):
+        for s in range(1, ring):
+            outbound(t, s, 0).wait_recv()
 
     def multiply(t):
+        for s in range(1, ring):
+            outbound(t, s, 1).wait_recv()
+
         @pl.when(t >= 2)
         def _():
             for s in range(1, ring):
@@ -273,8 +257,13 @@
         homeward_own(t).start()
 
     def finish(t):
-        own_load = pltpu.make_async_copy(pair_ref.at[:, part(t)], pair, load_sem.at[1])
+        own_load = pltpu.make_async_copy(pair_ref.at[:, :, part(t)], pair, load_sem.at[1])
         own_load.start()
+        own_load.wait()
+        for b in range(ring):
+            turn[b * tall : (b + 1) * tall, :] = (
+                pair[b].astype(jnp.float32).reshape(tall, channels)
+            )
         for s in range(1, ring):
             homeward(t, s).wait_recv()
 
@@ -289,30 +278,34 @@
         def _():
             keep(t - 1).wait()
 
-        own_load.wait()
         home_load.wait()
 
         def column(j, carry):
             for b in range(ring):
-                own = pair[b, j].astype(jnp.float32)
+                own = turn[pl.ds(b * tall + j, rows, stride=WIDTH), :]
                 normed = layer_norm(own).astype(jnp.bfloat16)
                 gate = jax.nn.sigmoid(
                     jnp.dot(normed, gate_ref[...], preferred_element_type=jnp.float32)
                 )
                 back = jnp.dot(home[b, j], out_ref[...], preferred_element_type=jnp.float32)
                 live = live_ref[b] * col_ref[b, t * WIDTH + j]
-                one = (own + live * gate * back).astype(jnp.bfloat16)
-                result[b, j] = one
-                size = jnp.abs(one.astype(jnp.float32)).reshape(rows // 8, 8, channels)
-                total_ref[...] += jnp.sum(size, axis=0)
+                one = (own + live * gate * back).astype(jnp.bfloat16).astype(jnp.float32)
+                turn[pl.ds(b * tall + j, rows, stride=WIDTH), :] = one
+                total_ref[...] += jnp.sum(jnp.abs(one).reshape(rows // 8, 8, channels), axis=0)
             return carry
 
         lax.fori_loop(0, WIDTH, column, 0, unroll=UNROLL)
+        for b in range(ring):
+            result[b] = (
+                turn[b * tall : (b + 1) * tall, :]
+                .reshape(rows, WIDTH, channels)
+                .astype(jnp.bfloat16)
+            )
         keep(t).start()
 
     lag = 3
 
-    def step(t, carry):
+    def spread(t, carry):
         @pl.when(t < steps)
         def _():
             multiply(t)
@@ -327,7 +320,7 @@
 
         return carry
 
-    lax.fori_loop(0, steps + lag, step, 0)
+    lax.fori_loop(0, steps + lag, spread, 0)
     sending = []
     for phase, (axis, size) in enumerate(axes):
         here = lax.axis_index(axis)
@@ -350,9 +343,13 @@
         copy.wait_send()
     keep(steps - 1).wait()
     for t in range(max(steps - 2, 0), steps):
+        drain(t)
         for s in range(1, ring):
             across(t, s).wait_send()
             homeward(t, s).wait_send()
+    for t in range(steps):
+        for s in range(1, ring):
+            inbound(t, s).wait_send()
 
 
 def rehomed(pair_repr, seq_lengths, weight_in, weight_out):
@@ -375,62 +372,44 @@
     row_live = ((row_first + row_local)[None, :] < lengths[:, None]).astype(jnp.float32)
     row_live = jnp.broadcast_to(row_live[:, :, None], (ring, rows, channels))
     col_live = (col_at[None, :] < lengths[:, None]).astype(jnp.float32)
-    pair_t = pair_repr.transpose(0, 2, 1, 3)
-    weight_t = weight_in[:, : 4 * hidden].T
     any_space = pl.BlockSpec(memory_space=pl.ANY)
     vmem = pl.BlockSpec(memory_space=pltpu.VMEM)
     smem = pl.BlockSpec(memory_space=pltpu.SMEM)
     dma = pltpu.SemaphoreType.DMA
     f32, bf16 = jnp.float32, jnp.bfloat16
 
-    sides, _ = pl.pallas_call(
-        functools.partial(enter_kernel, ring),
+    updated, total, _, _, _ = pl.pallas_call(
+        functools.partial(whole_kernel, ring, pairs),
         out_shape=(
-            jax.ShapeDtypeStruct((steps, ring, 2, quarter, WIDTH, deep), bf16),
-            jax.ShapeDtypeStruct((ring - 1, cols, rows, channels), bf16),
-        ),
-        in_specs=[any_space, vmem, vmem],
-        out_specs=(any_space, any_space),
-        scratch_shapes=[
-            pltpu.VMEM((WIDTH, deep, channels), bf16),
-            pltpu.VMEM((deep // LANES, 2 * hidden * WIDTH, LANES), f32),
-            pltpu.VMEM((2, ring, 2, quarter, WIDTH, deep), bf16),
-            dma((ring,)),
-            dma((steps, ring - 1)),
-            dma((steps, ring - 1)),
-            dma((steps, ring - 1)),
-            dma((steps, ring - 1)),
-            dma((steps,)),
-        ],
-        compiler_params=pltpu.CompilerParams(
-            collective_id=0, has_side_effects=True, vmem_limit_bytes=60 * 1024 * 1024
-        ),
-        name="enter",
-    )(pair_t, weight_t, mask)
-
-    updated_t, total, _, _ = pl.pallas_call(
-        functools.partial(leave_kernel, ring, pairs),
-        out_shape=(
-            jax.ShapeDtypeStruct(pair_t.shape, bf16),
+            jax.ShapeDtypeStruct(pair_repr.shape, bf16),
             jax.ShapeDtypeStruct((8, channels), f32),
+            jax.ShapeDtypeStruct((steps, ring - 1, rows, WIDTH, channels), bf16),
             jax.ShapeDtypeStruct((steps, ring, quarter, WIDTH, ring * rows), bf16),
             jax.ShapeDtypeStruct((ring, cols, rows, channels), bf16),
         ),
-        in_specs=[any_space, any_space, vmem, vmem, vmem, smem],
-        out_specs=(any_space, vmem, any_space, any_space),
+        in_specs=[any_space, vmem, vmem, vmem, vmem, vmem, smem],
+        out_specs=(any_space, vmem, any_space, any_space, any_space),
         scratch_shapes=[
+            pltpu.VMEM((deep, WIDTH, channels), bf16),
+            pltpu.VMEM((deep * WIDTH, channels), f32),
+            pltpu.VMEM((deep // LANES, 2 * hidden * WIDTH, LANES), f32),
+            pltpu.VMEM((2, ring, 2, quarter, WIDTH, deep), bf16),
             pltpu.VMEM((quarter, ring * cols, deep), bf16),
             pltpu.VMEM((quarter, ring * cols, deep), bf16),
             pltpu.VMEM((2, ring, quarter, WIDTH, ring * rows), bf16),
             pltpu.VMEM((ring, quarter, WIDTH, ring * rows), bf16),
-            pltpu.VMEM((ring * rows // LANES, hidden * WIDTH, LANES), f32),
             pltpu.VMEM((2, ring, WIDTH, rows, channels), bf16),
             pltpu.VMEM((ring, WIDTH, rows, channels), bf16),
-            pltpu.VMEM((ring, WIDTH, rows, channels), bf16),
-            pltpu.VMEM((ring, WIDTH, rows, channels), bf16),
+            pltpu.VMEM((ring, rows, WIDTH, channels), bf16),
+            pltpu.VMEM((ring, rows, WIDTH, channels), bf16),
             pltpu.VMEM((3, 8, channels), f32),
             pltpu.VMEM((3, most, 8, channels), f32),
-            dma((2,)),
+            dma((ring,)),
+            dma((steps, ring - 1)),
+            dma((steps, ring - 1)),
+            dma((steps, ring - 1, 2)),
+            dma((steps, ring - 1, 2)),
+            dma((steps, 2)),
             dma((steps, ring - 1)),
             dma((steps, ring - 1)),
             dma((steps,)),
@@ -440,15 +419,12 @@
             dma(()),
             dma((3, most - 1)),
             dma((3, most - 1)),
-            dma((steps, ring, 2)),
         ],
         compiler_params=pltpu.CompilerParams(
-            collective_id=1, has_side_effects=True, vmem_limit_bytes=60 * 1024 * 1024
+            collective_id=0, has_side_effects=True, vmem_limit_bytes=60 * 1024 * 1024
         ),
-        name="leave",
-    )(sides, pair_t, weight_in[:, 4 * hidden :], weight_out, row_live, col_live)
-
-    updated = updated_t.transpose(0, 2, 1, 3)
+        name="whole",
+    )(pair_repr, weight_in[:, : 4 * hidden].T, weight_in[:, 4 * hidden :], weight_out, mask, row_live, col_live)
     entry_count = ring * pairs * rows * ring * cols * lax.axis_size("gy") * channels
     return (updated, jnp.sum(total) / float(entry_count))
 

time: 582 us -> 522 us (0.90)
  Pallas kernels: 546 us -> 499 us
  local copies, waits for them, and re-layouts: 28 us -> 15.2 us
    pallas_call x2 -> x1, Pallas kernels: 546 us -> 499 us  [rehomed(): pl.pallas_call(functools.partial(whole_kernel, ring, pairs), out_shape=(j...]
    unnamed x3 -> x2, local copies, waits for them, and re-layouts: 22.9 us -> 10.2 us
where the time goes in v3:
time: 522 us; the launch traced here: 521 us
  Pallas kernels  499 us (96%)
  local copies, waits for them, and re-layouts  15.2 us (3%)
    pallas_call x1, Pallas kernels, rehomed(): pl.pallas_call(functools.partial(whole_kernel, ring, pairs), out_shape=(j...  499 us

profile of v3, /device:TPU:0, one launch (start us, length us, event | category | flops | bytes accessed | tf_op | source)
XLA Modules:
  0.0 521.1 jit_solution(17056870217012687966)
XLA Ops:
  0.7 1.2 dynamic_slice.10
  1.9 0.7 dynamic_slice.11
  2.6 0.7 add_compare_fusion
  3.4 0.7 broadcast_compare_fusion
  4.0 0.6 compare_convert_fusion
  4.7 1.4 slice.7.gate_ref
  6.0 0.9 slice.6
  7.0 0.8 copy.7
  7.7 0.7 and_convert_fusion.mask_ref
  8.5 0.8 broadcast_in_dim.2.live_ref
  9.2 499.4 %whole.1 = (bf16[4,96,96,128]{3,2,1,0:T(8,128)(2,1)}, f32[8,128]{1,0:T(8,128)}, bf16[6,3,96,16,128]{4,3,2,1,0:T(8,128)(2,1)}, bf16[6,4,32,16,384]{4,3,2,1,0:T(8,128)(2,1)}, bf16[4,96,96,128]{3,2,1,0:T(8,128)(2,1)}) custom-call(bf16[4,96,96,128]{3,2,1,0:T(8,128)(2,1)} %pair_ref.1, bf16[512,128]{1,0:T(8,128)(2,1)} %bitcast.2, bf16[128,128]{1,0:T(8,128)(2,1)} %slice.7.gate_ref, ...), custom_call_target="tpu_custom_call" | custom-call | tf_op jit(solution)/shard_map/whole/pallas_call | solution.py:381
  508.6 1.3 reduce_sum.9
  510.5 9.4 %copy.9 = bf16[4,96,96,128]{3,2,1,0:T(8,128)(2,1)} copy(bf16[4,96,96,128]{3,2,1,0:T(8,128)(2,1)} %get-tuple-element.14) | data formatting | bytes 18874368
  (3 shorter events, 0.0 us)

commit v4 on v3

--- a/solution.py
+++ b/solution.py
@@ -10,6 +10,7 @@
 WIDTH = 16
 UNROLL = 2
 WINDOW = 1
+AHEAD = 2
 LANES = 128
 EPS = 1e-05
 
@@ -83,9 +84,16 @@
             side_send.at[t, s - 1, side], side_recv.at[t, s - 1, side], "gy", target,
         )
 
+    inner = jnp.logical_and(me > 0, me < ring - 1)
     for t in range(min(WINDOW, steps)):
         for s in range(1, ring):
             inbound(t, s).start()
+
+    @pl.when(inner)
+    def _():
+        for t in range(WINDOW, min(AHEAD, steps)):
+            for s in range(1, ring):
+                inbound(t, s).start()
 
     def drain(t):
         for side in range(2):
@@ -96,10 +104,12 @@
         for s in range(1, ring):
             inbound(t, s).wait_recv()
 
-        @pl.when(t + WINDOW < steps)
-        def _():
-            for s in range(1, ring):
-                inbound(t + WINDOW, s).start()
+        for apart, window in ((inner, AHEAD), (jnp.logical_not(inner), WINDOW)):
+
+            @pl.when(jnp.logical_and(apart, t + window < steps))
+            def _():
+                for s in range(1, ring):
+                    inbound(t + window, s).start()
 
         loads = []
         for s in range(ring):

time: 522 us -> 517 us (level)
  no operation moved by 1% of the time
where the time goes in v4:
time: 517 us; the launch traced here: 516 us
  Pallas kernels  495 us (96%)
  local copies, waits for them, and re-layouts  15.2 us (3%)
    pallas_call x1, Pallas kernels, rehomed(): pl.pallas_call(functools.partial(whole_kernel, ring, pairs), out_shape=(j...  495 us

profile of v4, /device:TPU:0, one launch (start us, length us, event | category | flops | bytes accessed | tf_op | source)
XLA Modules:
  0.0 516.3 jit_solution(10676783303088333358)
XLA Ops:
  0.7 1.2 dynamic_slice.10
  1.9 0.7 dynamic_slice.11
  2.6 0.7 add_compare_fusion
  3.4 0.7 broadcast_compare_fusion
  4.0 0.6 compare_convert_fusion
  4.7 1.4 slice.7.gate_ref
  6.0 0.9 slice.6
  7.0 0.8 copy.7
  7.7 0.7 and_convert_fusion.mask_ref
  8.5 0.8 broadcast_in_dim.2.live_ref
  9.2 494.5 %whole.1 = (bf16[4,96,96,128]{3,2,1,0:T(8,128)(2,1)}, f32[8,128]{1,0:T(8,128)}, bf16[6,3,96,16,128]{4,3,2,1,0:T(8,128)(2,1)}, bf16[6,4,32,16,384]{4,3,2,1,0:T(8,128)(2,1)}, bf16[4,96,96,128]{3,2,1,0:T(8,128)(2,1)}) custom-call(bf16[4,96,96,128]{3,2,1,0:T(8,128)(2,1)} %pair_ref.1, bf16[512,128]{1,0:T(8,128)(2,1)} %bitcast.2, bf16[128,128]{1,0:T(8,128)(2,1)} %slice.7.gate_ref, ...), custom_call_target="tpu_custom_call" | custom-call | tf_op jit(solution)/shard_map/whole/pallas_call | solution.py:391
  503.8 1.3 reduce_sum.9
  505.7 9.4 %copy.9 = bf16[4,96,96,128]{3,2,1,0:T(8,128)(2,1)} copy(bf16[4,96,96,128]{3,2,1,0:T(8,128)(2,1)} %get-tuple-element.14) | data formatting | bytes 18874368
  (3 shorter events, 0.0 us)
